TPU v7x, 32 devices: a whole 2x2x4 slice. The times are simulated.
32 devices in a mesh: rep: 4 (over x, y), dp: 8 (over z, core).
Axes of the slice: x: 2, y: 2, z: 4, core: 2. Of those that a mesh axis runs over, the one named last changes fastest.
Arguments:
- g_w_gate: bfloat16 [32, 2, 1024, 4096], P(('rep', 'dp')), parts along dimension 0
- g_w_up: bfloat16 [32, 2, 1024, 4096], P(('rep', 'dp')), parts along dimension 0
- g_w_down: bfloat16 [32, 2, 4096, 1024], P(('rep', 'dp')), parts along dimension 0
- w_gate: bfloat16 [2, 1024, 4096], replicated
- w_up: bfloat16 [2, 1024, 4096], replicated
- w_down: bfloat16 [2, 4096, 1024], replicated
- m_w_gate: float32 [2, 1024, 4096], P(None, 'dp')
- m_w_up: float32 [2, 1024, 4096], P(None, 'dp')
- m_w_down: float32 [2, 4096, 1024], P(None, 'dp')
- v_w_gate: float32 [2, 1024, 4096], P(None, 'dp')
- v_w_up: float32 [2, 1024, 4096], P(None, 'dp')
- v_w_down: float32 [2, 4096, 1024], P(None, 'dp')
Outputs:
- output 1: bfloat16 [8, 1024, 4096], P('rep'), parts along dimension 0
- output 2: bfloat16 [8, 1024, 4096], P('rep'), parts along dimension 0
- output 3: bfloat16 [8, 4096, 1024], P('rep'), parts along dimension 0
- output 4: float32 [8, 1024, 4096], P('rep', 'dp'), parts along dimension 0
- output 5: float32 [8, 1024, 4096], P('rep', 'dp'), parts along dimension 0
- output 6: float32 [8, 4096, 1024], P('rep', 'dp'), parts along dimension 0
- output 7: float32 [8, 1024, 4096], P('rep', 'dp'), parts along dimension 0
- output 8: float32 [8, 1024, 4096], P('rep', 'dp'), parts along dimension 0
- output 9: float32 [8, 4096, 1024], P('rep', 'dp'), parts along dimension 0
There are 4 independent parts. A program takes and returns all parts, laid end to end along the dimension named above; an argument that names none is the same for every part.
All inputs are finite; a program needn't handle non-finite values.
Results may differ from a plain program's by a relative error of at most 0.022.
Values are sent between devices in bfloat16 or wider.
A program may use at most 2 GiB of HBM per device.

v0:
```python
import jax
import jax.numpy as jnp
from jax import lax
from jax.sharding import PartitionSpec as P


def adamw(w, m, v, g):
    m = 0.9 * m + 0.1 * g
    v = 0.95 * v + 0.05 * g * g
    step = m * lax.rsqrt(v + 1e-8) + 0.1 * w
    return (w - 0.02 * step).astype(jnp.bfloat16), m, v


def clipped(gradients, sum_of_squares, count):
    factor = jnp.minimum(1.0, 0.5 * lax.rsqrt(sum_of_squares / count + 1e-30))
    return [g * factor for g in gradients]


def solution(mesh):
    def step(*arrays):
        terms, weights, m, v = (arrays[i : i + 3] for i in (0, 3, 6, 9))
        gradients = [lax.psum_scatter(t[0], "dp", scatter_dimension=1, tiled=True).astype(jnp.float32) for t in terms]
        squares = lax.psum(sum(jnp.sum(g * g) for g in gradients), "dp")
        gradients = clipped(gradients, squares, lax.psum(1, "dp") * sum(g.size for g in gradients))
        me = lax.axis_index("dp")
        own = [lax.dynamic_slice_in_dim(w, me * one.shape[1], one.shape[1], 1).astype(jnp.float32) for w, one in zip(weights, m, strict=True)]
        new = [adamw(w, m, v, g) for w, m, v, g in zip(own, m, v, gradients, strict=True)]
        whole = [lax.all_gather(one[0], "dp", axis=1, tiled=True) for one in new]
        return (*whole, *(one[1] for one in new), *(one[2] for one in new))

    all_of, cut = P(None, None, None), P(None, "dp", None)
    return jax.shard_map(
        step,
        mesh=mesh,
        in_specs=(P(("rep", "dp"), None, None, None),) * 3 + (all_of,) * 3 + (cut,) * 6,
        out_specs=(P("rep", None, None),) * 3 + (P("rep", "dp", None),) * 6,
        check_vma=False,
    )
```

profile of v0, /device:TPU:0, one launch (start us, length us, event | category | flops | bytes accessed | tf_op | source)
XLA Modules:
  0.0 1040.5 jit_solution(13891633003180949659)
XLA Ops:
  7.2 0.7 reduce-scatter.4.cloned.1.call-update
  8.0 0.7 reduce-scatter.6.cloned.1.call-update
  8.7 0.7 reduce-scatter.8.cloned.1.call-update
  9.4 0.0 all-gather.8.cloned.1.call-start
  9.4 171.7 %reduce-scatter.4.cloned.1.call-done = bf16[2,128,4096]{2,1,0:T(8,128)(2,1)} async-done(((bf16[2,1024,4096]{2,1,0:T(8,128)(2,1)}), bf16[2,128,4096]{2,1,0:T(8,128)(2,1)}) %reduce-scatter.4.cloned.1.call-update) | async-done | bytes 2097168 | tf_op jit(solution)/shard_map/reduce_scatter | solution.py:22
  181.1 3.3 fusion.9
  184.4 165.9 %reduce-scatter.6.cloned.1.call-done = bf16[2,128,4096]{2,1,0:T(8,128)(2,1)} async-done(((bf16[2,1024,4096]{2,1,0:T(8,128)(2,1)}), bf16[2,128,4096]{2,1,0:T(8,128)(2,1)}) %reduce-scatter.6.cloned.1.call-update) | async-done | bytes 2097168 | tf_op jit(solution)/shard_map/reduce_scatter | solution.py:22
  350.2 3.3 fusion.10
  354.8 164.6 %reduce-scatter.8.cloned.1.call-done = bf16[2,512,1024]{2,1,0:T(8,128)(2,1)} async-done(((bf16[2,4096,1024]{2,1,0:T(8,128)(2,1)}), bf16[2,512,1024]{2,1,0:T(8,128)(2,1)}) %reduce-scatter.8.cloned.1.call-update) | async-done | bytes 2097168 | tf_op jit(solution)/shard_map/reduce_scatter | solution.py:22
  519.4 3.3 fusion.11
  523.3 14.3 %psum.7 = f32[]{:T(128)} all-reduce(f32[]{:T(128)S(6)} %add.65), channel_id=1, replica_groups=mesh['rep'=4,'dp'=8] {'dp'}, use_global_device_ids=true, to_apply=%region_6.0 | all-reduce | flops 1 | bytes 8 | tf_op jit(solution)/shard_map/psum | solution.py:23
  538.4 8.2 fusion.17
  546.5 0.0 all-gather.4.cloned.1.call-start
  546.6 8.4 fusion.8
  555.1 0.0 all-gather.6.cloned.1.call-start
  555.1 7.1 fusion.14
  562.2 133.8 %all-gather.8.cloned.1.call-done = bf16[2,4096,1024]{2,1,0:T(8,128)(2,1)} async-done(((bf16[2,512,1024]{2,1,0:T(8,128)(2,1)}), bf16[2,4096,1024]{2,1,0:T(8,128)(2,1)}) %all-gather.8.cloned.1.call-update) | async-done | bytes 16777232 | tf_op jit(solution)/shard_map/all_gather | solution.py:28
  696.0 151.8 %all-gather.4.cloned.1.call-done = bf16[2,1024,4096]{2,1,0:T(8,128)(2,1)} async-done(((bf16[2,128,4096]{2,1,0:T(8,128)(2,1)}), bf16[2,1024,4096]{2,1,0:T(8,128)(2,1)}) %all-gather.4.cloned.1.call-update) | async-done | bytes 16777232 | tf_op jit(solution)/shard_map/all_gather | solution.py:28
  847.8 151.8 %all-gather.6.cloned.1.call-done = bf16[2,1024,4096]{2,1,0:T(8,128)(2,1)} async-done(((bf16[2,128,4096]{2,1,0:T(8,128)(2,1)}), bf16[2,1024,4096]{2,1,0:T(8,128)(2,1)}) %all-gather.6.cloned.1.call-update) | async-done | bytes 16777232 | tf_op jit(solution)/shard_map/all_gather | solution.py:28
  999.6 16.8 %copy.24 = bf16[2,1024,4096]{2,1,0:T(8,128)(2,1)} copy(bf16[2,1024,4096]{2,1,0:T(8,128)(2,1)} %all-gather.4.cloned.1.call-done) | data formatting | bytes 33554432
  1016.4 8.5 copy.25
  1024.9 1.4 slice-done.2
  1026.3 1.2 slice-done.3
  1027.5 6.2 copy.26
  (17 shorter events, 0.2 us)
Async XLA Ops:
  7.2 173.9 %reduce-scatter.4.cloned.1.call-start = ((), (), s32[]{:S(2)}) async-start(), calls=%async_computation.3 | async-start | bytes 18874368 | tf_op jit(solution)/shard_map/reduce_scatter | solution.py:22
  7.9 342.3 %reduce-scatter.6.cloned.1.call-start = ((), (), s32[]{:S(2)}) async-start(), calls=%async_computation.4 | async-start | bytes 18874368 | tf_op jit(solution)/shard_map/reduce_scatter | solution.py:22
  8.7 510.7 %reduce-scatter.8.cloned.1.call-start = ((), (), s32[]{:S(2)}) async-start(), calls=%async_computation.5 | async-start | bytes 18874368 | tf_op jit(solution)/shard_map/reduce_scatter | solution.py:22
  9.4 686.6 %all-gather.8.cloned.1.call-start = ((), (), s32[]{:S(2)}) async-start(), calls=%async_computation.8 | async-start | bytes 18874368 | tf_op jit(solution)/shard_map/all_gather | solution.py:28
  546.5 301.3 %all-gather.4.cloned.1.call-start = ((), (), s32[]{:S(2)}) async-start(), calls=%async_computation.6 | async-start | bytes 18874368 | tf_op jit(solution)/shard_map/all_gather | solution.py:28
  546.6 8.5 copy-start.1
  555.1 444.5 %all-gather.6.cloned.1.call-start = ((), (), s32[]{:S(2)}) async-start(), calls=%async_computation.7 | async-start | bytes 18874368 | tf_op jit(solution)/shard_map/all_gather | solution.py:28
  999.6 16.8 %copy-start = (bf16[2,1024,4096]{2,1,0:T(8,128)(2,1)S(1)}, bf16[2,1024,4096]{2,1,0:T(8,128)(2,1)}, u32[]{:S(2)}) copy-start(bf16[2,1024,4096]{2,1,0:T(8,128)(2,1)} %all-gather.6.cloned.1.call-done) | copy-start | bytes 50331652
  999.6 25.3 %slice-start = ((s8[16777216]{0:T(1024)(128)(4,1)}), s8[4194304]{0:T(1024)(128)(4,1)S(1)}, s32[]{:S(2)}) async-start(s8[16777216]{0:T(1024)(128)(4,1)} %bitcast.6), calls=%async_computation.9 | async-start | bytes 8388608
  999.6 25.3 %slice-start.1 = ((s8[16777216]{0:T(1024)(128)(4,1)}), s8[4194304]{0:T(1024)(128)(4,1)S(1)}, s32[]{:S(2)}) async-start(s8[16777216]{0:T(1024)(128)(4,1)} %bitcast.6), calls=%async_computation.10 | async-start | bytes 8388608
  1016.4 9.9 slice-start.2
  1016.4 11.1 %slice-start.3 = ((s8[16777216]{0:T(1024)(128)(4,1)}), s8[4194304]{0:T(1024)(128)(4,1)S(1)}, s32[]{:S(2)}) async-start(s8[16777216]{0:T(1024)(128)(4,1)} %bitcast.6), calls=%async_computation.12 | async-start | bytes 8388608
Sparse Core Ops, SparseCore 0:
  10.3 170.7 reduce-scatter.3
  183.5 166.7 reduce-scatter.5
  352.6 166.7 reduce-scatter.7
  546.7 149.3 all-gather.7
  698.0 149.7 all-gather.3
  849.8 149.7 all-gather.5
where the time goes:
time: 1040 us
  waiting for transfers between devices  942 us (91%)
  local copies, waits for them, and re-layouts  34.1 us (3%)
  other arithmetic  33.5 us (3%)
  between operations  16.8 us (2%)
  blocking collectives  14.3 us (1%)
    reduce_scatter x3, waiting for transfers between devices, step(): lax.psum_scatter(t[0], 'dp', scatter_dimension=1, tiled=True)  502 us
    all_gather x3, waiting for transfers between devices, step(): whole = [lax.all_gather(one[0], 'dp', axis=1, tiled=True) for one in new]  437 us
    unnamed x15, local copies, waits for them, and re-layouts  34.1 us
    convert_element_type x3, other arithmetic, adamw(): return ((w - 0.02 * step).astype(jnp.bfloat16), m, v)  23.7 us
  transfers between devices with their start and end apart: 6, of which 6 were waited for; matrix products, arithmetic and copies ran while one was open for 2% of the time, Pallas kernels for 0%

commit v1 on v0

v1 whole, which is shorter than its diff:
```python
import functools
import math

import jax
import jax.numpy as jnp
from jax import lax
from jax.experimental import pallas as pl
from jax.experimental.pallas import tpu as pltpu
from jax.sharding import PartitionSpec as P

MESH = pl.DeviceIdType.MESH
CR, CC = 128, 1024
PER = 24
N = 2 * PER
S = 4
D = 2
ROWS = 16


def kernel(count, *refs):
    terms, weights, ms, vs = refs[0:3], refs[3:6], refs[6:9], refs[9:12]
    wo, mo, vo = refs[12:15], refs[15:18], refs[18:21]
    (own, par, up, snd, gbuf, acc, nrm, fac, mb, vb, wb, mq, vq,
     own_s, par_s, give_s, up_s, snd_s, par_c, up_c, g_s, gs_s, w_s, out_s, pr_s, ps_s, loc_s, in_s, mv_s, n_s, ns_s) = refs[21:]

    d = lax.axis_index("dp")
    z, c = d // 2, d % 2
    right = z >= 2
    is_end = (z == 0) | (z == 3)
    is_in = (z == 1) | (z == 2)
    mine = jnp.where(right, 2, 1)
    end = jnp.where(right, 3, 0)
    other = 3 - mine
    far = 3 - end
    partner = d + 1 - 2 * c

    def dev(zz):
        return {"dp": 2 * zz + c}

    buddy = {"dp": partner}

    def block_of(s, b):
        return 2 + b if s == 0 else 1 - b

    def by_array(i, fn):
        for a in range(3):
            @pl.when((i >= 8 * a) & (i < 8 * a + 8))
            def _():
                t = i - 8 * a
                fn(a, t // 4, t % 4)

    def whole(ref, a, layer, q, dd, lead=()):
        if a < 2:
            return ref.at[(*lead, layer, pl.ds(pl.multiple_of(dd * 128, 128), CR), pl.ds(pl.multiple_of(q * CC, CC), CC))]
        return ref.at[(*lead, layer, pl.ds(pl.multiple_of(dd * 512 + q * 128, 128), CR), pl.ds(0, CC))]

    def block(ref, a, layer, q):
        if a < 2:
            return ref.at[layer, pl.ds(0, CR), pl.ds(pl.multiple_of(q * CC, CC), CC)]
        return ref.at[layer, pl.ds(pl.multiple_of(q * 128, 128), CR), pl.ds(0, CC)]

    def wait(ref, sem):
        pltpu.make_async_copy(ref, ref, sem).wait()

    def remote(src, dst, ssem, rsem, to):
        return pltpu.make_async_remote_copy(src, dst, ssem, rsem, device_id=to, device_id_type=MESH)

    def start_own(s, j):
        slot = lax.rem(j, S)
        dd = 2 * block_of(s, j // PER) + c

        def go(a, layer, q):
            pltpu.make_async_copy(whole(terms[a], a, layer, q, dd, (0,)), own.at[s, slot], own_s.at[s, slot]).start()

        by_array(lax.rem(j, PER), go)

    def start_give(s, j):
        slot = lax.rem(j, S)
        dd = 2 * block_of(s, j // PER) + 1 - c

        def go(a, layer, q):
            remote(whole(terms[a], a, layer, q, dd, (0,)), par.at[s, slot], give_s.at[s, slot], par_s.at[s, slot], buddy).start()

        by_array(lax.rem(j, PER), go)

    for s in range(2):
        for j in range(S):
            start_own(s, jnp.int32(j))

    barrier = pltpu.get_barrier_semaphore()
    for k in range(1, 8):
        pl.semaphore_signal(barrier, inc=1, device_id={"dp": lax.rem(d + k, 8)}, device_id_type=MESH)
    pl.semaphore_wait(barrier, 7)

    for s in range(2):
        for j in range(S):
            start_give(s, jnp.int32(j))

    acc[...] = jnp.zeros_like(acc)

    def rows(fn):
        def go(r, carry):
            fn(pl.ds(pl.multiple_of(r * ROWS, ROWS), ROWS))
            return carry

        lax.fori_loop(0, CR // ROWS, go, 0)

    def f32(x):
        return x.astype(jnp.float32)

    def process(s, k):
        zz = z if s == 0 else 3 - z
        down = z + 1 if s == 0 else z - 1
        above = z - 1 if s == 0 else z + 1
        j = k - D * zz

        @pl.when((j >= 0) & (j < N))
        def _():
            slot = lax.rem(j, S)
            wait(own.at[s, slot], own_s.at[s, slot])
            wait(par.at[s, slot], par_s.at[s, slot])

            @pl.when((zz < 3) & (j >= S))
            def _():
                wait(snd.at[s, slot], snd_s.at[s, slot])

            @pl.when(zz == 0)
            def _():
                def add(r):
                    snd[s, slot, r, :] = (f32(own[s, slot, r, :]) + f32(par[s, slot, r, :])).astype(jnp.bfloat16)

                rows(add)

            @pl.when(zz > 0)
            def _():
                wait(up.at[s, slot], up_s.at[s, slot])

            @pl.when((zz > 0) & (zz < 3))
            def _():
                def add(r):
                    snd[s, slot, r, :] = (f32(up[s, slot, r, :]) + (f32(own[s, slot, r, :]) + f32(par[s, slot, r, :]))).astype(jnp.bfloat16)

                rows(add)

            @pl.when(zz == 3)
            def _():
                def add(r):
                    g = (f32(up[s, slot, r, :]) + (f32(own[s, slot, r, :]) + f32(par[s, slot, r, :]))).astype(jnp.bfloat16)
                    gbuf[j, r, :] = g
                    acc[...] += f32(g) * f32(g)

                rows(add)

            @pl.when(j < N - S)
            def _():
                pl.semaphore_signal(par_c.at[s], inc=1, device_id=buddy, device_id_type=MESH)

            @pl.when((zz > 0) & (j < N - S))
            def _():
                pl.semaphore_signal(up_c.at[s], inc=1, device_id=dev(above), device_id_type=MESH)

            @pl.when(j + S < N)
            def _():
                start_own(s, j + S)

            @pl.when(zz < 3)
            def _():
                @pl.when(j >= S)
                def _():
                    pl.semaphore_wait(up_c.at[s], 1)

                remote(snd.at[s, slot], up.at[s, slot], snd_s.at[s, slot], up_s.at[s, slot], dev(down)).start()

            @pl.when((j >= 1) & (j + S - 1 < N))
            def _():
                again = lax.rem(j + S - 1, S)
                pl.semaphore_wait(par_c.at[s], 1)
                wait(par.at[s, again], give_s.at[s, again])
                start_give(s, j + S - 1)

    def send_sums():
        def go(i, carry):
            remote(gbuf.at[i], gbuf.at[i], gs_s, g_s.at[i], dev(mine)).start()
            return carry

        lax.fori_loop(0, PER, go, 0)

    def step(k, carry):
        process(0, k)
        process(1, k)

        @pl.when(is_end & (k == N))
        def _():
            send_sums()

        return carry

    lax.fori_loop(0, N + 3 * D, step, 0)

    def start_mvw(i):
        slot = lax.rem(i, 2)

        def go(a, layer, q):
            pltpu.make_async_copy(block(ms[a], a, layer, q), mb.at[slot], in_s.at[slot, 0]).start()
            pltpu.make_async_copy(block(vs[a], a, layer, q), vb.at[slot], in_s.at[slot, 1]).start()
            pltpu.make_async_copy(whole(weights[a], a, layer, q, d), wb.at[slot], in_s.at[slot, 2]).start()

        by_array(i, go)

    start_mvw(jnp.int32(0))

    slot_of = jnp.where(right, 2, 0) + c

    @pl.when(is_end)
    def _():
        part = acc[0:8, 0:128]
        for r in range(ROWS // 8):
            for q in range(CC // 128):
                if r + q:
                    part = part + acc[8 * r : 8 * r + 8, 128 * q : 128 * q + 128]
        nrm[slot_of] = part
        for k in range(1, 8):
            remote(nrm.at[slot_of], nrm.at[slot_of], ns_s.at[k], n_s.at[slot_of], {"dp": lax.rem(d + k, 8)}).start()

    for s in range(2):
        for q in range(S):
            wait(par.at[s, q], give_s.at[s, q])
        zz = z if s == 0 else 3 - z

        @pl.when(zz < 3)
        def _():
            for q in range(S):
                wait(snd.at[s, q], snd_s.at[s, q])

    for k in range(4):
        @pl.when(jnp.logical_not(is_end & (slot_of == k)))
        def _():
            wait(nrm.at[k], n_s.at[k])

    total = jnp.sum((nrm[0] + nrm[1]) + (nrm[2] + nrm[3]), keepdims=True)
    fac[...] = jnp.broadcast_to(jnp.minimum(1.0, 0.5 * lax.rsqrt(total / count + 1e-30)), fac.shape)

    base = jnp.where(is_end, PER, 0)

    def update(i, carry):
        slot = lax.rem(i, 2)
        at = base + i

        @pl.when(i + 1 < PER)
        def _():
            start_mvw(i + 1)

        wait(mb.at[slot], in_s.at[slot, 0])
        wait(vb.at[slot], in_s.at[slot, 1])
        wait(wb.at[slot], in_s.at[slot, 2])

        @pl.when(i >= 2)
        def _():
            wait(mq.at[slot], mv_s.at[slot, 0])
            wait(vq.at[slot], mv_s.at[slot, 1])

        @pl.when(is_in)
        def _():
            wait(gbuf.at[i], g_s.at[i])

        def adam(r):
            g = f32(gbuf[at, r, :]) * fac[...]
            m = 0.9 * mb[slot, r, :] + 0.1 * g
            v = 0.95 * vb[slot, r, :] + 0.05 * g * g
            w = f32(wb[slot, r, :])
            mq[slot, r, :] = m
            vq[slot, r, :] = v
            gbuf[at, r, :] = (w - 0.02 * (m * lax.rsqrt(v + 1e-8) + 0.1 * w)).astype(jnp.bfloat16)

        rows(adam)

        def go(a, layer, q):
            new = gbuf.at[at]
            there = whole(wo[a], a, layer, q, d)
            pltpu.make_async_copy(mq.at[slot], block(mo[a], a, layer, q), mv_s.at[slot, 0]).start()
            pltpu.make_async_copy(vq.at[slot], block(vo[a], a, layer, q), mv_s.at[slot, 1]).start()

            @pl.when(is_end)
            def _():
                remote(new, there, out_s.at[0], w_s.at[z, i], dev(mine)).start()

            @pl.when(is_in)
            def _():
                remote(new, there, out_s.at[0], w_s.at[z, i], dev(end)).start()
                remote(new, there, out_s.at[1], w_s.at[z, i], dev(other)).start()

            remote(new, there, ps_s.at[z], pr_s.at[z], buddy).start()
            pltpu.make_async_copy(new, there, loc_s).start()

        by_array(i, go)
        return carry

    lax.fori_loop(0, PER, update, 0)

    def pass_on(i, src, over):
        def go(a, layer, q):
            here = whole(wo[a], a, layer, q, 2 * src + c)
            wait(here, w_s.at[src, i])
            if over is not None:
                remote(here, here, out_s.at[over[0]], w_s.at[src, i], dev(over[1])).start()
            remote(here, here, ps_s.at[src], pr_s.at[src], buddy).start()

        by_array(i, go)

    @pl.when(is_in)
    def _():
        def one(i, carry):
            pass_on(i, other, (3, end))
            pass_on(i, end, (2, other))
            return carry

        lax.fori_loop(0, PER, one, 0)

        def two(i, carry):
            pass_on(i, far, (4, end))
            return carry

        lax.fori_loop(0, PER, two, 0)

    @pl.when(is_end)
    def _():
        for src in (mine, other, far):
            def one(i, carry):
                pass_on(i, src, None)
                return carry

            lax.fori_loop(0, PER, one, 0)

    for slot in range(2):
        wait(mq.at[slot], mv_s.at[slot, 0])
        wait(vq.at[slot], mv_s.at[slot, 1])
    six = gbuf.at[pl.ds(0, PER)]
    wait(six, loc_s)
    wait(six, out_s.at[0])

    @pl.when(is_in)
    def _():
        for k in range(1, 5):
            wait(six, out_s.at[k])

    @pl.when(is_end)
    def _():
        wait(six, gs_s)
        for k in range(1, 8):
            wait(nrm.at[slot_of], ns_s.at[k])

    for k in range(4):
        wait(six, ps_s.at[k])
        wait(six, pr_s.at[k])


def solution(mesh):
    def step(*arrays):
        weights, m = arrays[3:6], arrays[6:9]
        count = float(8 * sum(math.prod(a.shape) for a in m))
        any_ = pl.BlockSpec(memory_space=pl.ANY)
        chunk = (CR, CC)
        dma, regular = pltpu.SemaphoreType.DMA, pltpu.SemaphoreType.REGULAR
        out = [jax.ShapeDtypeStruct(w.shape, jnp.bfloat16) for w in weights] + [jax.ShapeDtypeStruct(a.shape, jnp.float32) for a in m] * 2
        return pl.pallas_call(
            functools.partial(kernel, count),
            out_shape=out,
            in_specs=[any_] * 12,
            out_specs=[any_] * 9,
            scratch_shapes=[
                pltpu.VMEM((2, S, *chunk), jnp.bfloat16),
                pltpu.VMEM((2, S, *chunk), jnp.bfloat16),
                pltpu.VMEM((2, S, *chunk), jnp.bfloat16),
                pltpu.VMEM((2, S, *chunk), jnp.bfloat16),
                pltpu.VMEM((N, *chunk), jnp.bfloat16),
                pltpu.VMEM((ROWS, CC), jnp.float32),
                pltpu.VMEM((4, 8, 128), jnp.float32),
                pltpu.VMEM((1, CC), jnp.float32),
                pltpu.VMEM((2, *chunk), jnp.float32),
                pltpu.VMEM((2, *chunk), jnp.float32),
                pltpu.VMEM((2, *chunk), jnp.bfloat16),
                pltpu.VMEM((2, *chunk), jnp.float32),
                pltpu.VMEM((2, *chunk), jnp.float32),
                dma((2, S)),
                dma((2, S)),
                dma((2, S)),
                dma((2, S)),
                dma((2, S)),
                regular((2,)),
                regular((2,)),
                dma((PER,)),
                dma,
                dma((4, PER)),
                dma((5,)),
                dma((4,)),
                dma((4,)),
                dma,
                dma((2, 3)),
                dma((2, 2)),
                dma((4,)),
                dma((8,)),
            ],
            compiler_params=pltpu.CompilerParams(collective_id=0, has_side_effects=True, vmem_limit_bytes=40 * 2**20),
            cost_estimate=pl.CostEstimate(flops=10**9, bytes_accessed=3 * 10**8, transcendentals=3 * 2**20),
        )(*arrays)

    all_of, cut = P(None, None, None), P(None, "dp", None)
    return jax.shard_map(
        step,
        mesh=mesh,
        in_specs=(P(("rep", "dp"), None, None, None),) * 3 + (all_of,) * 3 + (cut,) * 6,
        out_specs=(P("rep", None, None),) * 3 + (P("rep", "dp", None),) * 6,
        check_vma=False,
    )
```

time: 1040 us -> 880 us (0.85)
  waiting for transfers between devices: 942 us -> 0 us
  Pallas kernels: 0 us -> 824 us
  other arithmetic: 33.5 us -> 0.01 us
  local copies, waits for them, and re-layouts: 34.1 us -> 53.9 us
  between operations: 16.8 us -> 0.7 us
  blocking collectives: 14.3 us -> 0 us
    pallas_call x0 -> x1, Pallas kernels: none -> 824 us  [step(): pl.pallas_call(functools.partial(kernel, count), out_shape=out, in_specs=...]
    reduce_scatter x3 -> x0, waiting for transfers between devices: 502 us -> none  [step(): lax.psum_scatter(t[0], 'dp', scatter_dimension=1, tiled=True)]
    all_gather x3 -> x0, waiting for transfers between devices: 437 us -> none  [step(): whole = [lax.all_gather(one[0], 'dp', axis=1, tiled=True) for one in new]]
    convert_element_type x3 -> x0, other arithmetic: 23.7 us -> none  [adamw(): return ((w - 0.02 * step).astype(jnp.bfloat16), m, v)]
    unnamed x15 -> x23, local copies, waits for them, and re-layouts: 34.1 us -> 53.9 us
    psum x1 -> x0, blocking collectives: 14.3 us -> none  [step(): squares = lax.psum(sum((jnp.sum(g * g) for g in gradients)), 'dp')]
  transfers between devices with their start and end apart: 6 -> 0, of which waited for: 6 -> 0; matrix products, arithmetic and copies ran while one was open for 2% -> 0% of each run, Pallas kernels for 0% -> 0%
where the time goes in v1:
time: 880 us; the launch traced here: 879 us
  Pallas kernels  824 us (94%)
  local copies, waits for them, and re-layouts  53.9 us (6%)
    pallas_call x1, Pallas kernels, step(): pl.pallas_call(functools.partial(kernel, count), out_shape=out, in_specs=...  824 us
    unnamed x23, local copies, waits for them, and re-layouts  53.9 us

profile of v1, /device:TPU:0, one launch (start us, length us, event | category | flops | bytes accessed | tf_op | source)
XLA Modules:
  0.0 878.8 jit_solution(6336963619783563435)
XLA Ops:
  0.6 824.2 %shard_map.187 = (bf16[2,1024,4096]{2,1,0:T(8,128)(2,1)}, bf16[2,1024,4096]{2,1,0:T(8,128)(2,1)}, bf16[2,4096,1024]{2,1,0:T(8,128)(2,1)}, f32[2,128,4096]{2,1,0:...) custom-call(bf16[1,2,1024,4096]{3,2,1,0:T(8,128)(2,1)} %refs_0_.1, ...), custom_call_target="tpu_custom_call" | custom-call | flops 1000000000 | bytes 300000000 | tf_op jit(solution)/shard_map/pallas_call | solution.py:365
  824.8 0.0 slice-start
  824.8 0.0 slice-start.1
  824.8 15.3 %copy.30 = bf16[2,1024,4096]{2,1,0:T(8,128)(2,1)} copy(bf16[2,1024,4096]{2,1,0:T(8,128)(2,1)} %get-tuple-element.18) | data formatting | bytes 33554432
  840.1 0.0 slice-start.2
  840.1 0.0 slice-start.3
  840.1 15.3 %copy.31 = bf16[2,1024,4096]{2,1,0:T(8,128)(2,1)} copy(bf16[2,1024,4096]{2,1,0:T(8,128)(2,1)} %get-tuple-element.19) | data formatting | bytes 33554432
  855.4 0.0 slice-done
  855.4 0.0 slice-done.1
  855.4 0.0 slice-done.2
  855.4 0.0 slice-done.3
  855.5 6.2 copy.32
  861.6 2.0 copy.33
  863.6 2.0 copy.34
  865.6 0.0 copy-start.2
  865.6 2.1 copy.35
  867.8 1.6 copy-done.2
  869.3 0.0 copy-start.1
  869.4 2.1 copy.36
  871.5 1.6 copy-done.1
  873.1 0.0 copy-start
  873.1 2.1 copy.37
  875.2 1.6 copy-done
  876.8 2.0 copy.38
  (1 shorter events, 0.0 us)
Async XLA Ops:
  824.8 30.6 %slice-start = ((s8[16777216]{0:T(1024)(128)(4,1)}), s8[4194304]{0:T(1024)(128)(4,1)S(1)}, s32[]{:S(2)}) async-start(s8[16777216]{0:T(1024)(128)(4,1)} %bitcast), calls=%async_computation | async-start | bytes 8388608
  824.8 30.6 %slice-start.1 = ((s8[16777216]{0:T(1024)(128)(4,1)}), s8[4194304]{0:T(1024)(128)(4,1)S(1)}, s32[]{:S(2)}) async-start(s8[16777216]{0:T(1024)(128)(4,1)} %bitcast), calls=%async_computation.1 | async-start | bytes 8388608
  840.1 15.3 %slice-start.2 = ((s8[16777216]{0:T(1024)(128)(4,1)}), s8[4194304]{0:T(1024)(128)(4,1)S(1)}, s32[]{:S(2)}) async-start(s8[16777216]{0:T(1024)(128)(4,1)} %bitcast), calls=%async_computation.2 | async-start | bytes 8388608
  840.1 15.3 %slice-start.3 = ((s8[16777216]{0:T(1024)(128)(4,1)}), s8[4194304]{0:T(1024)(128)(4,1)S(1)}, s32[]{:S(2)}) async-start(s8[16777216]{0:T(1024)(128)(4,1)} %bitcast), calls=%async_computation.3 | async-start | bytes 8388608
  865.6 3.7 copy-start.2
  869.3 3.7 copy-start.1
  873.1 3.7 copy-start

commit v2 on v1

--- a/solution.py
+++ b/solution.py
@@ -14,6 +14,9 @@
 N = 2 * PER
 S = 4
 D = 2
+W = 3
+AHEAD = 3 * D
+LAG = 3
 ROWS = 16
 
 
@@ -21,7 +24,7 @@
     terms, weights, ms, vs = refs[0:3], refs[3:6], refs[6:9], refs[9:12]
     wo, mo, vo = refs[12:15], refs[15:18], refs[18:21]
     (own, par, up, snd, gbuf, acc, nrm, fac, mb, vb, wb, mq, vq,
-     own_s, par_s, give_s, up_s, snd_s, par_c, up_c, g_s, gs_s, w_s, out_s, pr_s, ps_s, loc_s, in_s, mv_s, n_s, ns_s) = refs[21:]
+     own_s, par_s, give_s, up_s, snd_s, par_c, up_c, g_s, w_s, out_s, pr_s, ps_s, loc_s, in_s, mv_s, n_s, ns_s) = refs[21:]
 
     d = lax.axis_index("dp")
     z, c = d // 2, d % 2
@@ -178,20 +181,22 @@
                 wait(par.at[s, again], give_s.at[s, again])
                 start_give(s, j + S - 1)
 
-    def send_sums():
-        def go(i, carry):
-            remote(gbuf.at[i], gbuf.at[i], gs_s, g_s.at[i], dev(mine)).start()
-            return carry
-
-        lax.fori_loop(0, PER, go, 0)
+    def room(link, u):
+        @pl.when(u >= W)
+        def _():
+            wait(gbuf.at[0], out_s.at[link, lax.rem(u, W)])
+
+    def send_sum(u):
+        room(0, u)
+        remote(gbuf.at[u], gbuf.at[u], out_s.at[0, lax.rem(u, W)], g_s.at[u], dev(mine)).start()
 
     def step(k, carry):
         process(0, k)
         process(1, k)
 
-        @pl.when(is_end & (k == N))
-        def _():
-            send_sums()
+        @pl.when(is_end & (k >= N))
+        def _():
+            send_sum(k - N)
 
         return carry
 
@@ -242,7 +247,7 @@
 
     base = jnp.where(is_end, PER, 0)
 
-    def update(i, carry):
+    def update(i):
         slot = lax.rem(i, 2)
         at = base + i
 
@@ -274,78 +279,112 @@
 
         rows(adam)
 
+        @pl.when(is_in)
+        def _():
+            room(0, i)
+            room(1, i)
+
         def go(a, layer, q):
             new = gbuf.at[at]
             there = whole(wo[a], a, layer, q, d)
             pltpu.make_async_copy(mq.at[slot], block(mo[a], a, layer, q), mv_s.at[slot, 0]).start()
             pltpu.make_async_copy(vq.at[slot], block(vo[a], a, layer, q), mv_s.at[slot, 1]).start()
 
-            @pl.when(is_end)
-            def _():
-                remote(new, there, out_s.at[0], w_s.at[z, i], dev(mine)).start()
-
             @pl.when(is_in)
             def _():
-                remote(new, there, out_s.at[0], w_s.at[z, i], dev(end)).start()
-                remote(new, there, out_s.at[1], w_s.at[z, i], dev(other)).start()
+                remote(new, there, out_s.at[0, lax.rem(i, W)], w_s.at[z, i], dev(end)).start()
+                remote(new, there, out_s.at[1, lax.rem(i, W)], w_s.at[z, i], dev(other)).start()
 
             remote(new, there, ps_s.at[z], pr_s.at[z], buddy).start()
             pltpu.make_async_copy(new, there, loc_s).start()
 
         by_array(i, go)
-        return carry
-
-    lax.fori_loop(0, PER, update, 0)
+
+    def send_new(i, u):
+        room(0, u)
+
+        def go(a, layer, q):
+            remote(gbuf.at[PER + i], whole(wo[a], a, layer, q, d), out_s.at[0, lax.rem(u, W)], w_s.at[z, i], dev(mine)).start()
+
+        by_array(i, go)
 
     def pass_on(i, src, over):
+        if over is not None:
+            room(over[0], over[1])
+
         def go(a, layer, q):
             here = whole(wo[a], a, layer, q, 2 * src + c)
             wait(here, w_s.at[src, i])
             if over is not None:
-                remote(here, here, out_s.at[over[0]], w_s.at[src, i], dev(over[1])).start()
+                remote(here, here, out_s.at[over[0], lax.rem(over[1], W)], w_s.at[src, i], dev(over[2])).start()
             remote(here, here, ps_s.at[src], pr_s.at[src], buddy).start()
 
         by_array(i, go)
 
     @pl.when(is_in)
     def _():
-        def one(i, carry):
-            pass_on(i, other, (3, end))
-            pass_on(i, end, (2, other))
+        def first(t, carry):
+            update(t)
             return carry
 
-        lax.fori_loop(0, PER, one, 0)
-
-        def two(i, carry):
-            pass_on(i, far, (4, end))
+        lax.fori_loop(0, PER, first, 0)
+
+        def second(i, carry):
+            pass_on(i, other, (0, PER + i, end))
+            pass_on(i, end, (1, PER + i, other))
             return carry
 
-        lax.fori_loop(0, PER, two, 0)
+        lax.fori_loop(0, PER, second, 0)
+
+        def third(i, carry):
+            pass_on(i, far, (0, 2 * PER + i, end))
+            return carry
+
+        lax.fori_loop(0, PER, third, 0)
 
     @pl.when(is_end)
     def _():
-        for src in (mine, other, far):
-            def one(i, carry):
-                pass_on(i, src, None)
-                return carry
-
-            lax.fori_loop(0, PER, one, 0)
+        def tick(t, carry):
+            u = t + AHEAD
+
+            @pl.when(u < PER)
+            def _():
+                send_sum(u)
+
+            @pl.when(t < PER)
+            def _():
+                update(t)
+
+            @pl.when((u >= PER) & (u < 2 * PER))
+            def _():
+                send_new(u - PER, u)
+
+            got = t - LAG
+
+            @pl.when((got >= 0) & (got < 3 * PER))
+            def _():
+                which = got // PER
+                pass_on(lax.rem(got, PER), jnp.where(which == 0, mine, jnp.where(which == 1, other, far)), None)
+
+            return carry
+
+        lax.fori_loop(0, 3 * PER + LAG, tick, 0)
 
     for slot in range(2):
         wait(mq.at[slot], mv_s.at[slot, 0])
         wait(vq.at[slot], mv_s.at[slot, 1])
     six = gbuf.at[pl.ds(0, PER)]
     wait(six, loc_s)
-    wait(six, out_s.at[0])
+    for k in range(W):
+        wait(gbuf.at[0], out_s.at[0, k])
 
     @pl.when(is_in)
     def _():
-        for k in range(1, 5):
-            wait(six, out_s.at[k])
+        for k in range(W):
+            wait(gbuf.at[0], out_s.at[1, k])
 
     @pl.when(is_end)
     def _():
-        wait(six, gs_s)
         for k in range(1, 8):
             wait(nrm.at[slot_of], ns_s.at[k])
 
@@ -389,9 +428,8 @@
                 regular((2,)),
                 regular((2,)),
                 dma((PER,)),
-                dma,
                 dma((4, PER)),
-                dma((5,)),
+                dma((2, W)),
                 dma((4,)),
                 dma((4,)),
                 dma,

time: 880 us -> 778 us (0.88)
  Pallas kernels: 824 us -> 723 us
    pallas_call x1, Pallas kernels: 824 us -> 723 us  [step(): pl.pallas_call(functools.partial(kernel, count), out_shape=out, in_specs=...]
where the time goes in v2:
time: 778 us
  Pallas kernels  723 us (93%)
  local copies, waits for them, and re-layouts  53.9 us (7%)
    pallas_call x1, Pallas kernels, step(): pl.pallas_call(functools.partial(kernel, count), out_shape=out, in_specs=...  723 us
    unnamed x23, local copies, waits for them, and re-layouts  53.9 us

profile of v2, /device:TPU:0, one launch (start us, length us, event | category | flops | bytes accessed | tf_op | source)
XLA Modules:
  0.0 777.6 jit_solution(2551530960397910110)
XLA Ops:
  0.6 723.0 %shard_map.187 = (bf16[2,1024,4096]{2,1,0:T(8,128)(2,1)}, bf16[2,1024,4096]{2,1,0:T(8,128)(2,1)}, bf16[2,4096,1024]{2,1,0:T(8,128)(2,1)}, f32[2,128,4096]{2,1,0:...) custom-call(bf16[1,2,1024,4096]{3,2,1,0:T(8,128)(2,1)} %refs_0_.1, ...), custom_call_target="tpu_custom_call" | custom-call | flops 1000000000 | bytes 300000000 | tf_op jit(solution)/shard_map/pallas_call | solution.py:404
  723.7 0.0 slice-start
  723.7 0.0 slice-start.1
  723.7 15.3 %copy.30 = bf16[2,1024,4096]{2,1,0:T(8,128)(2,1)} copy(bf16[2,1024,4096]{2,1,0:T(8,128)(2,1)} %get-tuple-element.18) | data formatting | bytes 33554432
  739.0 0.0 slice-start.2
  739.0 0.0 slice-start.3
  739.0 15.3 %copy.31 = bf16[2,1024,4096]{2,1,0:T(8,128)(2,1)} copy(bf16[2,1024,4096]{2,1,0:T(8,128)(2,1)} %get-tuple-element.19) | data formatting | bytes 33554432
  754.3 0.0 slice-done
  754.3 0.0 slice-done.1
  754.3 0.0 slice-done.2
  754.3 0.0 slice-done.3
  754.3 6.2 copy.32
  760.5 2.0 copy.33
  762.5 2.0 copy.34
  764.5 0.0 copy-start.2
  764.5 2.1 copy.35
  766.7 1.6 copy-done.2
  768.2 0.0 copy-start.1
  768.2 2.1 copy.36
  770.4 1.6 copy-done.1
  771.9 0.0 copy-start
  771.9 2.1 copy.37
  774.1 1.6 copy-done
  775.6 2.0 copy.38
  (1 shorter events, 0.0 us)
Async XLA Ops:
  723.7 30.6 %slice-start = ((s8[16777216]{0:T(1024)(128)(4,1)}), s8[4194304]{0:T(1024)(128)(4,1)S(1)}, s32[]{:S(2)}) async-start(s8[16777216]{0:T(1024)(128)(4,1)} %bitcast), calls=%async_computation | async-start | bytes 8388608
  723.7 30.6 %slice-start.1 = ((s8[16777216]{0:T(1024)(128)(4,1)}), s8[4194304]{0:T(1024)(128)(4,1)S(1)}, s32[]{:S(2)}) async-start(s8[16777216]{0:T(1024)(128)(4,1)} %bitcast), calls=%async_computation.1 | async-start | bytes 8388608
  739.0 15.3 %slice-start.2 = ((s8[16777216]{0:T(1024)(128)(4,1)}), s8[4194304]{0:T(1024)(128)(4,1)S(1)}, s32[]{:S(2)}) async-start(s8[16777216]{0:T(1024)(128)(4,1)} %bitcast), calls=%async_computation.2 | async-start | bytes 8388608
  739.0 15.3 %slice-start.3 = ((s8[16777216]{0:T(1024)(128)(4,1)}), s8[4194304]{0:T(1024)(128)(4,1)S(1)}, s32[]{:S(2)}) async-start(s8[16777216]{0:T(1024)(128)(4,1)} %bitcast), calls=%async_computation.3 | async-start | bytes 8388608
  764.5 3.7 copy-start.2
  768.2 3.7 copy-start.1
  771.9 3.7 copy-start

commit v3 on v2

--- a/solution.py
+++ b/solution.py
@@ -17,14 +17,29 @@
 W = 3
 AHEAD = 3 * D
 LAG = 3
+X = 12
 ROWS = 16
+
+
+def by_array(i, fn):
+    for a in range(3):
+        @pl.when((i >= 8 * a) & (i < 8 * a + 8))
+        def _():
+            t = i - 8 * a
+            fn(a, t // 4, t % 4)
+
+
+def whole(ref, a, layer, q, dd, lead=()):
+    if a < 2:
+        return ref.at[(*lead, layer, pl.ds(pl.multiple_of(dd * 128, 128), CR), pl.ds(pl.multiple_of(q * CC, CC), CC))]
+    return ref.at[(*lead, layer, pl.ds(pl.multiple_of(dd * 512 + q * 128, 128), CR), pl.ds(0, CC))]
 
 
 def kernel(count, *refs):
     terms, weights, ms, vs = refs[0:3], refs[3:6], refs[6:9], refs[9:12]
-    wo, mo, vo = refs[12:15], refs[15:18], refs[18:21]
+    wo, mo, vo, tail = refs[12:15], refs[15:18], refs[18:21], refs[21]
     (own, par, up, snd, gbuf, acc, nrm, fac, mb, vb, wb, mq, vq,
-     own_s, par_s, give_s, up_s, snd_s, par_c, up_c, g_s, w_s, out_s, pr_s, ps_s, loc_s, in_s, mv_s, n_s, ns_s) = refs[21:]
+     own_s, par_s, give_s, up_s, snd_s, par_c, up_c, g_s, w_s, out_s, pr_s, ps_s, loc_s, in_s, mv_s, n_s, ns_s) = refs[22:]
 
     d = lax.axis_index("dp")
     z, c = d // 2, d % 2
@@ -45,18 +60,6 @@
     def block_of(s, b):
         return 2 + b if s == 0 else 1 - b
 
-    def by_array(i, fn):
-        for a in range(3):
-            @pl.when((i >= 8 * a) & (i < 8 * a + 8))
-            def _():
-                t = i - 8 * a
-                fn(a, t // 4, t % 4)
-
-    def whole(ref, a, layer, q, dd, lead=()):
-        if a < 2:
-            return ref.at[(*lead, layer, pl.ds(pl.multiple_of(dd * 128, 128), CR), pl.ds(pl.multiple_of(q * CC, CC), CC))]
-        return ref.at[(*lead, layer, pl.ds(pl.multiple_of(dd * 512 + q * 128, 128), CR), pl.ds(0, CC))]
-
     def block(ref, a, layer, q):
         if a < 2:
             return ref.at[layer, pl.ds(0, CR), pl.ds(pl.multiple_of(q * CC, CC), CC)]
@@ -316,8 +319,27 @@
             here = whole(wo[a], a, layer, q, 2 * src + c)
             wait(here, w_s.at[src, i])
             if over is not None:
-                remote(here, here, out_s.at[over[0], lax.rem(over[1], W)], w_s.at[src, i], dev(over[2])).start()
+                sems = out_s.at[over[0], lax.rem(over[1], W)], w_s.at[src, i]
+                if over[0] == 0:
+                    remote(here, here, *sems, dev(over[2])).start()
+                else:
+                    @pl.when(i < PER - X)
+                    def _():
+                        remote(here, here, *sems, dev(over[2])).start()
+
+                    @pl.when(i >= PER - X)
+                    def _():
+                        remote(here, tail.at[jnp.maximum(i - (PER - X), 0)], *sems, dev(over[2])).start()
+
             remote(here, here, ps_s.at[src], pr_s.at[src], buddy).start()
+
+        by_array(i, go)
+
+    def pass_tail(i):
+        def go(a, layer, q):
+            here = tail.at[i - (PER - X)]
+            wait(here, w_s.at[far, i])
+            remote(here, whole(wo[a], a, layer, q, 2 * far + c), ps_s.at[far], pr_s.at[far], buddy).start()
 
         by_array(i, go)
 
@@ -340,7 +362,13 @@
             pass_on(i, far, (0, 2 * PER + i, end))
             return carry
 
-        lax.fori_loop(0, PER, third, 0)
+        lax.fori_loop(0, PER - X, third, 0)
+
+        def fourth(i, carry):
+            pass_tail(i)
+            return carry
+
+        lax.fori_loop(PER - X, PER, fourth, 0)
 
     @pl.when(is_end)
     def _():
@@ -361,14 +389,14 @@
 
             got = t - LAG
 
-            @pl.when((got >= 0) & (got < 3 * PER))
+            @pl.when((got >= 0) & (got < 3 * PER - X))
             def _():
                 which = got // PER
                 pass_on(lax.rem(got, PER), jnp.where(which == 0, mine, jnp.where(which == 1, other, far)), None)
 
             return carry
 
-        lax.fori_loop(0, 3 * PER + LAG, tick, 0)
+        lax.fori_loop(0, 3 * PER - X + LAG, tick, 0)
 
     for slot in range(2):
         wait(mq.at[slot], mv_s.at[slot, 0])
@@ -389,8 +417,95 @@
             wait(nrm.at[slot_of], ns_s.at[k])
 
     for k in range(4):
-        wait(six, ps_s.at[k])
-        wait(six, pr_s.at[k])
+        less = is_end & (far == k)
+
+        @pl.when(less)
+        def _():
+            part = gbuf.at[pl.ds(0, PER - X)]
+            wait(part, ps_s.at[k])
+            wait(part, pr_s.at[k])
+
+        @pl.when(jnp.logical_not(less))
+        def _():
+            wait(six, ps_s.at[k])
+            wait(six, pr_s.at[k])
+
+
+def copies(*refs):
+    src, dst, buf, sem_in, sem_out = refs[0:9], refs[9:18], refs[18:22], refs[22], refs[23]
+    items = []
+    for a in range(9):
+        down, layers, rows_ = a % 3 == 2, src[a].shape[0], src[a].shape[1]
+        kind = (1 if down else 0) + (0 if a < 3 else 2)
+        size = buf[kind].shape[1]
+        items += [(a, kind, layer, r, size) for layer in range(layers) for r in range(0, rows_, size)]
+    n = len(items)
+    used = [[0] * 4, []]
+    slots = []
+    for it in items:
+        slots.append(used[0][it[1]] % 3)
+        used[0][it[1]] += 1
+    last = {}
+
+    def start_in(k):
+        a, kind, layer, r, size = items[k]
+        key = (kind, slots[k])
+        if key in last:
+            out(last[key]).wait()
+        last[key] = k
+        inn(k).start()
+
+    def inn(k):
+        a, kind, layer, r, size = items[k]
+        return pltpu.make_async_copy(src[a].at[layer, pl.ds(r, size)], buf[kind].at[slots[k]], sem_in.at[kind, slots[k]])
+
+    def out(k):
+        a, kind, layer, r, size = items[k]
+        return pltpu.make_async_copy(buf[kind].at[slots[k]], dst[a].at[layer, pl.ds(r, size)], sem_out.at[kind, slots[k]])
+
+    for k in range(2):
+        start_in(k)
+    for k in range(n):
+        inn(k).wait()
+        out(k).start()
+        if k + 2 < n:
+            start_in(k + 2)
+    for k in last.values():
+        out(k).wait()
+
+
+def place(tail, one, two, *refs):
+    dst, buf, sem_in, sem_out = refs[3:6], refs[6], refs[7], refs[8]
+    d = lax.axis_index("dp")
+    z, c = d // 2, d % 2
+    is_in = (z == 1) | (z == 2)
+    far = jnp.where(z >= 2, 0, 3)
+
+    @pl.when(is_in)
+    def _():
+        pltpu.make_async_copy(tail, buf.at[0], sem_in.at[0]).start()
+
+    @pl.when(jnp.logical_not(is_in))
+    def _():
+        pltpu.make_async_copy(one, buf.at[0], sem_in.at[0]).start()
+        pltpu.make_async_copy(two, buf.at[1], sem_in.at[1]).start()
+
+    def put(which, core):
+        pltpu.make_async_copy(one, buf.at[which], sem_in.at[which]).wait()
+        for k in range(X):
+            i = PER - X + k
+            a = i // 8
+            there = whole(dst[a], a, (i % 8) // 4, i % 4, 2 * far + core)
+            pltpu.make_async_copy(buf.at[which, k], there, sem_out.at[which]).start()
+
+    put(0, c)
+
+    @pl.when(jnp.logical_not(is_in))
+    def _():
+        put(1, 1 - c)
+        pltpu.make_async_copy(one, buf.at[1], sem_out.at[1]).wait()
+
+    pltpu.make_async_copy(one, buf.at[0], sem_out.at[0]).wait()
 
 
 def solution(mesh):
@@ -401,11 +516,12 @@
         chunk = (CR, CC)
         dma, regular = pltpu.SemaphoreType.DMA, pltpu.SemaphoreType.REGULAR
         out = [jax.ShapeDtypeStruct(w.shape, jnp.bfloat16) for w in weights] + [jax.ShapeDtypeStruct(a.shape, jnp.float32) for a in m] * 2
-        return pl.pallas_call(
+        last = jax.ShapeDtypeStruct((X, *chunk), jnp.bfloat16)
+        *first, tail = pl.pallas_call(
             functools.partial(kernel, count),
-            out_shape=out,
+            out_shape=[*out, last],
             in_specs=[any_] * 12,
-            out_specs=[any_] * 9,
+            out_specs=[any_] * 10,
             scratch_shapes=[
                 pltpu.VMEM((2, S, *chunk), jnp.bfloat16),
                 pltpu.VMEM((2, S, *chunk), jnp.bfloat16),
@@ -441,6 +557,35 @@
             compiler_params=pltpu.CompilerParams(collective_id=0, has_side_effects=True, vmem_limit_bytes=40 * 2**20),
             cost_estimate=pl.CostEstimate(flops=10**9, bytes_accessed=3 * 10**8, transcendentals=3 * 2**20),
         )(*arrays)
+        one = lax.ppermute(tail, "dp", [(2, 0), (3, 1), (4, 6), (5, 7)])
+        copied = pl.pallas_call(
+            copies,
+            out_shape=out,
+            in_specs=[any_] * 9,
+            out_specs=[any_] * 9,
+            scratch_shapes=[
+                pltpu.VMEM((3, 256, 4096), jnp.bfloat16),
+                pltpu.VMEM((3, 1024, 1024), jnp.bfloat16),
+                pltpu.VMEM((3, 128, 4096), jnp.float32),
+                pltpu.VMEM((3, 512, 1024), jnp.float32),
+                dma((4, 3)),
+                dma((4, 3)),
+            ],
+            compiler_params=pltpu.CompilerParams(vmem_limit_bytes=32 * 2**20),
+            cost_estimate=pl.CostEstimate(flops=4 * 10**8, bytes_accessed=150 * 2**20, transcendentals=0),
+        )(*first)
+        one, *copied = lax.optimization_barrier((one, *copied))
+        two = lax.ppermute(one, "dp", [(0, 1), (1, 0), (6, 7), (7, 6)])
+        new = pl.pallas_call(
+            place,
+            out_shape=out[:3],
+            in_specs=[any_] * 6,
+            out_specs=[any_] * 3,
+            input_output_aliases={3: 0, 4: 1, 5: 2},
+            scratch_shapes=[pltpu.VMEM((2, X, *chunk), jnp.bfloat16), dma((2,)), dma((2,))],
+            compiler_params=pltpu.CompilerParams(vmem_limit_bytes=16 * 2**20),
+        )(tail, one, two, *copied[:3])
+        return (*new, *copied[3:])
 
     all_of, cut = P(None, None, None), P(None, "dp", None)
     return jax.shard_map(

time: 778 us -> 740 us (0.951)
  local copies, waits for them, and re-layouts: 53.9 us -> 6.56 us
  waiting for transfers between devices: 0 us -> 20.8 us
  Pallas kernels: 723 us -> 708 us
    unnamed x23 -> x6, local copies, waits for them, and re-layouts: 53.9 us -> 6.56 us
    ppermute x0 -> x2, waiting for transfers between devices: none -> 20.8 us  [the longest x1 15.2 us: step(): one = lax.ppermute(tail, 'dp', [(2, 0), (3, 1), (4, 6), (5, 7)])]
    pallas_call x1 -> x3, Pallas kernels: 723 us -> 708 us  [the longest x1 656 us: step(): pl.pallas_call(functools.partial(kernel, count), out_shape=[*out, last],...]
  transfers between devices with their start and end apart: 0 -> 2, of which waited for: 0 -> 2; matrix products, arithmetic and copies ran while one was open for 0% -> 0% of each run, Pallas kernels for 0% -> 7%
where the time goes in v3:
time: 740 us; the launch traced here: 739 us
  Pallas kernels  708 us (96%)
  waiting for transfers between devices  20.8 us (3%)
    pallas_call x1, Pallas kernels, step(): pl.pallas_call(functools.partial(kernel, count), out_shape=[*out, last],...  656 us
    pallas_call x1, Pallas kernels, step(): pl.pallas_call(copies, out_shape=out, in_specs=[any_] * 9, out_specs=[any...  49.2 us
    ppermute x1, waiting for transfers between devices, step(): one = lax.ppermute(tail, 'dp', [(2, 0), (3, 1), (4, 6), (5, 7)])  15.2 us
  transfers between devices with their start and end apart: 2, of which 2 were waited for; matrix products, arithmetic and copies ran while one was open for 0% of the time, Pallas kernels for 7%

profile of v3, /device:TPU:0, one launch (start us, length us, event | category | flops | bytes accessed | tf_op | source)
XLA Modules:
  0.0 739.1 jit_solution(23071329039327231)
XLA Ops:
  0.6 655.6 %shard_map.187 = (bf16[2,1024,4096]{2,1,0:T(8,128)(2,1)}, bf16[2,1024,4096]{2,1,0:T(8,128)(2,1)}, bf16[2,4096,1024]{2,1,0:T(8,128)(2,1)}, f32[2,128,4096]{2,1,0:...) custom-call(bf16[1,2,1024,4096]{3,2,1,0:T(8,128)(2,1)} %refs_0_.1, ...), custom_call_target="tpu_custom_call" | custom-call | flops 1000000000 | bytes 300000000 | tf_op jit(solution)/shard_map/pallas_call | solution.py:520
  656.3 1.3 collective-permute-start
  657.6 0.0 copy-start
  657.6 2.2 copy-done
  659.8 0.0 copy-start.1
  659.8 2.2 copy-done.1
  662.0 0.0 copy-start.2
  662.0 2.2 copy-done.2
  664.1 49.2 %shard_map.188 = (bf16[2,1024,4096]{2,1,0:T(8,128)(2,1)}, bf16[2,1024,4096]{2,1,0:T(8,128)(2,1)}, bf16[2,4096,1024]{2,1,0:T(8,128)(2,1)}, f32[2,128,4096]{2,1,0:...) custom-call(bf16[2,1024,4096]{2,1,0:T(8,128)(2,1)} %get-tuple-elemen, ...), custom_call_target="tpu_custom_call" | custom-call | flops 400000000 | bytes 157286400 | tf_op jit(solution)/shard_map/pallas_call | solution.py:561
  713.3 15.2 %collective-permute-done.one = bf16[12,128,1024]{2,1,0:T(8,128)(2,1)S(1)} collective-permute-done((bf16[12,128,1024]{2,1,0:T(8,128)(2,1)S(1)}, bf16[12,128,1024]{2,1,0:T(8,128)(2,1)S(1)}, u32[]{:S(2)}, u32[]{:S(2)}) %collective-permute-start) | collective-permute-done | bytes 3145760 | tf_op jit(solution)/shard_map/ppermute | solution.py:560
  728.5 1.9 collective-permute-start.1
  730.4 5.6 collective-permute-done.1.two
  736.0 3.1 shard_map.189
Async XLA Ops:
  656.3 72.2 %collective-permute-start = (bf16[12,128,1024]{2,1,0:T(8,128)(2,1)S(1)}, bf16[12,128,1024]{2,1,0:T(8,128)(2,1)S(1)}, u32[]{:S(2)}, u32[]{:S(2)}) collective-permute-start(bf16[12,128,1024]{2,1,0:T(8,128)(2,1)S(1)} %get-tuple-element.41.tail), channel_id=1, source_target_pairs={{2,0},{3,1},{4,6},{5,7},{10,8},{11,9},{12,14},{13,15},{18,16},{19,... | collective-permute-start | bytes 9437192 | tf_op jit(solution)/shard_map/ppermute | solution.py:560
  657.6 2.2 copy-start
  659.8 2.2 copy-start.1
  662.0 2.2 copy-start.2
  728.5 7.5 %collective-permute-start.1 = (bf16[12,128,1024]{2,1,0:T(8,128)(2,1)S(1)}, bf16[12,128,1024]{2,1,0:T(8,128)(2,1)S(1)}, u32[]{:S(2)}, u32[]{:S(2)}) collective-permute-start(bf16[12,128,1024]{2,1,0:T(8,128)(2,1)S(1)} %collective-permute-done.one), channel_id=1, source_target_pairs={{0,1},{1,0},{6,7},{7,6},{8,9},{9,8},{14,15},{15,14},{16,17},{17,16... | collective-permute-start | bytes 9437192 | tf_op jit(solution)/shard_map/ppermute | solution.py:578

commit v4 on v3

--- a/solution.py
+++ b/solution.py
@@ -13,11 +13,13 @@
 PER = 24
 N = 2 * PER
 S = 4
+LOCAL = 8
+GUEST = PER - LOCAL
 D = 2
 W = 3
-AHEAD = 3 * D
+AHEAD = 2 * D
 LAG = 3
-X = 12
+X = 8
 ROWS = 16
 
 
@@ -38,10 +40,10 @@
 def kernel(count, *refs):
     terms, weights, ms, vs = refs[0:3], refs[3:6], refs[6:9], refs[9:12]
     wo, mo, vo, tail = refs[12:15], refs[15:18], refs[18:21], refs[21]
-    (own, par, up, snd, gbuf, acc, nrm, fac, mb, vb, wb, mq, vq,
-     own_s, par_s, give_s, up_s, snd_s, par_c, up_c, g_s, w_s, out_s, pr_s, ps_s, loc_s, in_s, mv_s, n_s, ns_s) = refs[22:]
-
-    d = lax.axis_index("dp")
+    (own, par, up, snd, ext, pre, gbuf, acc, nrm, fac, mb, vb, wb, mq, vq,
+     own_s, par_s, give_s, up_s, snd_s, par_c, up_c, g_s, ext_s, pre_s, pf_s, w_s, out_s, pr_s, ps_s, loc_s, in_s, mv_s, n_s, ns_s) = refs[22:]
+
+    d, group = lax.axis_index("dp"), lax.axis_index("rep")
     z, c = d // 2, d % 2
     right = z >= 2
     is_end = (z == 0) | (z == 3)
@@ -57,8 +59,13 @@
 
     buddy = {"dp": partner}
 
-    def block_of(s, b):
-        return 2 + b if s == 0 else 1 - b
+    def chunk_of(s, n):
+        zz = z if s == 0 else 3 - z
+        m = jnp.where(zz == 3, jnp.where(n < 4, N - LOCAL + n, jnp.where(n < N - 4, n - 4, n)), n)
+        late = m >= N - LOCAL
+        b = jnp.where((m >= GUEST) & jnp.logical_not(late), 1, 0)
+        i = jnp.where(late, m - (N - PER), m - b * GUEST)
+        return (2 + b if s == 0 else 1 - b), b, i
 
     def block(ref, a, layer, q):
         if a < 2:
@@ -73,21 +80,23 @@
 
     def start_own(s, j):
         slot = lax.rem(j, S)
-        dd = 2 * block_of(s, j // PER) + c
+        home, _, i = chunk_of(s, j)
+        dd = 2 * home + c
 
         def go(a, layer, q):
             pltpu.make_async_copy(whole(terms[a], a, layer, q, dd, (0,)), own.at[s, slot], own_s.at[s, slot]).start()
 
-        by_array(lax.rem(j, PER), go)
+        by_array(i, go)
 
     def start_give(s, j):
         slot = lax.rem(j, S)
-        dd = 2 * block_of(s, j // PER) + 1 - c
+        home, _, i = chunk_of(s, j)
+        dd = 2 * home + 1 - c
 
         def go(a, layer, q):
             remote(whole(terms[a], a, layer, q, dd, (0,)), par.at[s, slot], give_s.at[s, slot], par_s.at[s, slot], buddy).start()
 
-        by_array(lax.rem(j, PER), go)
+        by_array(i, go)
 
     for s in range(2):
         for j in range(S):
@@ -96,7 +105,9 @@
     barrier = pltpu.get_barrier_semaphore()
     for k in range(1, 8):
         pl.semaphore_signal(barrier, inc=1, device_id={"dp": lax.rem(d + k, 8)}, device_id_type=MESH)
-    pl.semaphore_wait(barrier, 7)
+    for k in range(1, 4):
+        pl.semaphore_signal(barrier, inc=1, device_id={"rep": lax.rem(group + k, 4)}, device_id_type=MESH)
+    pl.semaphore_wait(barrier, 10)
 
     for s in range(2):
         for j in range(S):
@@ -118,50 +129,64 @@
         zz = z if s == 0 else 3 - z
         down = z + 1 if s == 0 else z - 1
         above = z - 1 if s == 0 else z + 1
-        j = k - D * zz
+        j = k - jnp.where(zz == 3, 3 * D - 4, D * zz)
 
         @pl.when((j >= 0) & (j < N))
         def _():
             slot = lax.rem(j, S)
+            _, b, i = chunk_of(s, j)
+            back = (zz == 3) & ((j < 4) | (j >= N - 4))
+            here = (zz == 2) & (j >= N - LOCAL)
+            root = (zz == 3) & jnp.logical_not(back)
+            on = (zz < 3) & jnp.logical_not(here)
             wait(own.at[s, slot], own_s.at[s, slot])
             wait(par.at[s, slot], par_s.at[s, slot])
 
-            @pl.when((zz < 3) & (j >= S))
+            @pl.when((on & (j >= S)) | (back & (j >= N - 4)))
             def _():
                 wait(snd.at[s, slot], snd_s.at[s, slot])
 
-            @pl.when(zz == 0)
+            @pl.when((zz > 0) & jnp.logical_not(back))
+            def _():
+                wait(up.at[s, slot], up_s.at[s, slot])
+
+            def two(r):
+                return f32(own[s, slot, r, :]) + f32(par[s, slot, r, :])
+
+            @pl.when((zz == 0) | back)
             def _():
                 def add(r):
-                    snd[s, slot, r, :] = (f32(own[s, slot, r, :]) + f32(par[s, slot, r, :])).astype(jnp.bfloat16)
+                    snd[s, slot, r, :] = two(r).astype(jnp.bfloat16)
 
                 rows(add)
 
-            @pl.when(zz > 0)
-            def _():
-                wait(up.at[s, slot], up_s.at[s, slot])
-
-            @pl.when((zz > 0) & (zz < 3))
+            @pl.when((zz > 0) & on)
             def _():
                 def add(r):
-                    snd[s, slot, r, :] = (f32(up[s, slot, r, :]) + (f32(own[s, slot, r, :]) + f32(par[s, slot, r, :]))).astype(jnp.bfloat16)
+                    snd[s, slot, r, :] = (f32(up[s, slot, r, :]) + two(r)).astype(jnp.bfloat16)
 
                 rows(add)
 
-            @pl.when(zz == 3)
-            def _():
-                def add(r):
-                    g = (f32(up[s, slot, r, :]) + (f32(own[s, slot, r, :]) + f32(par[s, slot, r, :]))).astype(jnp.bfloat16)
-                    gbuf[j, r, :] = g
-                    acc[...] += f32(g) * f32(g)
-
-                rows(add)
+            def keep(r, total):
+                g = total.astype(jnp.bfloat16)
+                gbuf[b * PER + i, r, :] = g
+                acc[...] += f32(g) * f32(g)
+
+            @pl.when(root)
+            def _():
+                rows(lambda r: keep(r, f32(up[s, slot, r, :]) + two(r)))
+
+            @pl.when(here)
+            def _():
+                e = i - GUEST
+                wait(ext.at[e], ext_s.at[e])
+                rows(lambda r: keep(r, f32(up[s, slot, r, :]) + two(r) + f32(ext[e, r, :])))
 
             @pl.when(j < N - S)
             def _():
                 pl.semaphore_signal(par_c.at[s], inc=1, device_id=buddy, device_id_type=MESH)
 
-            @pl.when((zz > 0) & (j < N - S))
+            @pl.when(((zz > 0) & (zz < 3) & (j < N - S)) | (root & (j < N - LOCAL + 4 - S)))
             def _():
                 pl.semaphore_signal(up_c.at[s], inc=1, device_id=dev(above), device_id_type=MESH)
 
@@ -169,13 +194,18 @@
             def _():
                 start_own(s, j + S)
 
-            @pl.when(zz < 3)
+            @pl.when(on)
             def _():
                 @pl.when(j >= S)
                 def _():
                     pl.semaphore_wait(up_c.at[s], 1)
 
                 remote(snd.at[s, slot], up.at[s, slot], snd_s.at[s, slot], up_s.at[s, slot], dev(down)).start()
+
+            @pl.when(back)
+            def _():
+                e = jnp.maximum(i - GUEST, 0)
+                remote(snd.at[s, slot], ext.at[e], snd_s.at[s, slot], ext_s.at[e], dev(above)).start()
 
             @pl.when((j >= 1) & (j + S - 1 < N))
             def _():
@@ -184,6 +214,23 @@
                 wait(par.at[s, again], give_s.at[s, again])
                 start_give(s, j + S - 1)
 
+    def bring(h):
+        i, kind = 4 * (h // 2) + group, lax.rem(h, 2)
+
+        def go(a, layer, q):
+            for which, ref in enumerate((ms[a], vs[a])):
+                @pl.when(kind == which)
+                def _():
+                    remote(block(ref, a, layer, q), pre.at[i, which], pf_s, pre_s.at[i, which], dev(end)).start()
+
+        by_array(i, go)
+
+    def share(h):
+        i, kind = 4 * (h // 2) + group, lax.rem(h, 2)
+        wait(pre.at[i, kind], pre_s.at[i, kind])
+        for k in range(1, 4):
+            remote(pre.at[i, kind], pre.at[i, kind], pf_s, pre_s.at[i, kind], {"rep": lax.rem(group + k, 4)}).start()
+
     def room(link, u):
         @pl.when(u >= W)
         def _():
@@ -194,19 +241,34 @@
         remote(gbuf.at[u], gbuf.at[u], out_s.at[0, lax.rem(u, W)], g_s.at[u], dev(mine)).start()
 
     def step(k, carry):
+        @pl.when(is_in & (k < 4))
+        def _():
+            bring(k)
+
         process(0, k)
         process(1, k)
 
+        @pl.when(is_in & (k >= N - 4) & (k < N))
+        def _():
+            bring(k - (N - 8))
+
+        @pl.when(is_end & (k >= 4) & (k < 8))
+        def _():
+            share(k - 4)
+
         @pl.when(is_end & (k >= N))
         def _():
             send_sum(k - N)
 
         return carry
 
-    lax.fori_loop(0, N + 3 * D, step, 0)
-
-    def start_mvw(i):
-        slot = lax.rem(i, 2)
+    lax.fori_loop(0, N + 2 * D, step, 0)
+
+    def order(t):
+        return jnp.where(t < LOCAL, GUEST + t, t - LOCAL)
+
+    def start_mvw(t, i):
+        slot = lax.rem(t, 2)
 
         def go(a, layer, q):
             pltpu.make_async_copy(block(ms[a], a, layer, q), mb.at[slot], in_s.at[slot, 0]).start()
@@ -215,77 +277,89 @@
 
         by_array(i, go)
 
-    start_mvw(jnp.int32(0))
-
-    slot_of = jnp.where(right, 2, 0) + c
-
-    @pl.when(is_end)
-    def _():
-        part = acc[0:8, 0:128]
-        for r in range(ROWS // 8):
-            for q in range(CC // 128):
-                if r + q:
-                    part = part + acc[8 * r : 8 * r + 8, 128 * q : 128 * q + 128]
-        nrm[slot_of] = part
-        for k in range(1, 8):
-            remote(nrm.at[slot_of], nrm.at[slot_of], ns_s.at[k], n_s.at[slot_of], {"dp": lax.rem(d + k, 8)}).start()
+    start_mvw(jnp.int32(0), jnp.where(is_end, 0, GUEST))
+
+    part = acc[0:8, 0:128]
+    for r in range(ROWS // 8):
+        for q in range(CC // 128):
+            if r + q:
+                part = part + acc[8 * r : 8 * r + 8, 128 * q : 128 * q + 128]
+    nrm[d] = part
+    for k in range(1, 8):
+        remote(nrm.at[d], nrm.at[d], ns_s.at[k], n_s.at[d], {"dp": lax.rem(d + k, 8)}).start()
 
     for s in range(2):
         for q in range(S):
             wait(par.at[s, q], give_s.at[s, q])
-        zz = z if s == 0 else 3 - z
-
-        @pl.when(zz < 3)
-        def _():
-            for q in range(S):
-                wait(snd.at[s, q], snd_s.at[s, q])
-
-    for k in range(4):
-        @pl.when(jnp.logical_not(is_end & (slot_of == k)))
+        for q in range(S):
+            wait(snd.at[s, q], snd_s.at[s, q])
+
+    for k in range(8):
+        @pl.when(d != k)
         def _():
             wait(nrm.at[k], n_s.at[k])
 
-    total = jnp.sum((nrm[0] + nrm[1]) + (nrm[2] + nrm[3]), keepdims=True)
+    total = ((nrm[0] + nrm[1]) + (nrm[2] + nrm[3])) + ((nrm[4] + nrm[5]) + (nrm[6] + nrm[7]))
+    total = jnp.sum(total, keepdims=True)
     fac[...] = jnp.broadcast_to(jnp.minimum(1.0, 0.5 * lax.rsqrt(total / count + 1e-30)), fac.shape)
 
     base = jnp.where(is_end, PER, 0)
 
-    def update(i):
-        slot = lax.rem(i, 2)
+    def start_guest(t):
+        slot = lax.rem(t, 2)
+
+        def go(a, layer, q):
+            pltpu.make_async_copy(whole(weights[a], a, layer, q, 2 * mine + c), wb.at[slot], in_s.at[slot, 2]).start()
+
+        by_array(t - PER, go)
+
+    def adam(g, m, v, w):
+        g = f32(g) * fac[...]
+        m = 0.9 * m + 0.1 * g
+        v = 0.95 * v + 0.05 * g * g
+        w = f32(w)
+        return m, v, (w - 0.02 * (m * lax.rsqrt(v + 1e-8) + 0.1 * w)).astype(jnp.bfloat16)
+
+    def update(t, i):
+        slot = lax.rem(t, 2)
         at = base + i
 
-        @pl.when(i + 1 < PER)
-        def _():
-            start_mvw(i + 1)
+        @pl.when(t + 1 < PER)
+        def _():
+            start_mvw(t + 1, jnp.where(is_end, i + 1, order(t + 1)))
+
+        @pl.when(is_end & (t + 1 == PER))
+        def _():
+            start_guest(t + 1)
 
         wait(mb.at[slot], in_s.at[slot, 0])
         wait(vb.at[slot], in_s.at[slot, 1])
         wait(wb.at[slot], in_s.at[slot, 2])
 
-        @pl.when(i >= 2)
+        @pl.when(t >= 2)
         def _():
             wait(mq.at[slot], mv_s.at[slot, 0])
             wait(vq.at[slot], mv_s.at[slot, 1])
 
-        @pl.when(is_in)
+        @pl.when(is_in & (i < GUEST))
         def _():
             wait(gbuf.at[i], g_s.at[i])
 
-        def adam(r):
-            g = f32(gbuf[at, r, :]) * fac[...]
-            m = 0.9 * mb[slot, r, :] + 0.1 * g
-            v = 0.95 * vb[slot, r, :] + 0.05 * g * g
-            w = f32(wb[slot, r, :])
+        def new_rows(r):
+            m, v, w = adam(gbuf[at, r, :], mb[slot, r, :], vb[slot, r, :], wb[slot, r, :])
             mq[slot, r, :] = m
             vq[slot, r, :] = v
-            gbuf[at, r, :] = (w - 0.02 * (m * lax.rsqrt(v + 1e-8) + 0.1 * w)).astype(jnp.bfloat16)
-
-        rows(adam)
+            gbuf[at, r, :] = w
+
+        rows(new_rows)
 
         @pl.when(is_in)
         def _():
-            room(0, i)
-            room(1, i)
+            room(1, t)
+
+        @pl.when(is_in & (t < LOCAL))
+        def _():
+            room(0, t)
 
         def go(a, layer, q):
             new = gbuf.at[at]
@@ -295,10 +369,41 @@
 
             @pl.when(is_in)
             def _():
-                remote(new, there, out_s.at[0, lax.rem(i, W)], w_s.at[z, i], dev(end)).start()
-                remote(new, there, out_s.at[1, lax.rem(i, W)], w_s.at[z, i], dev(other)).start()
+                remote(new, there, out_s.at[1, lax.rem(t, W)], w_s.at[z, i], dev(other)).start()
+
+            @pl.when(is_in & (t < LOCAL))
+            def _():
+                remote(new, there, out_s.at[0, lax.rem(t, W)], w_s.at[z, i], dev(end)).start()
 
             remote(new, there, ps_s.at[z], pr_s.at[z], buddy).start()
+            pltpu.make_async_copy(new, there, loc_s).start()
+
+        by_array(i, go)
+
+    def update_guest(t):
+        slot = lax.rem(t, 2)
+        i = t - PER
+
+        @pl.when(t + 1 < PER + GUEST)
+        def _():
+            start_guest(t + 1)
+
+        wait(wb.at[slot], in_s.at[slot, 2])
+
+        @pl.when(lax.rem(i, 4) != group)
+        def _():
+            wait(pre.at[i, 0], pre_s.at[i, 0])
+            wait(pre.at[i, 1], pre_s.at[i, 1])
+
+        def new_rows(r):
+            gbuf[i, r, :] = adam(gbuf[i, r, :], pre[i, 0, r, :], pre[i, 1, r, :], wb[slot, r, :])[2]
+
+        rows(new_rows)
+
+        def go(a, layer, q):
+            new = gbuf.at[i]
+            there = whole(wo[a], a, layer, q, 2 * mine + c)
+            remote(new, there, ps_s.at[mine], pr_s.at[mine], buddy).start()
             pltpu.make_async_copy(new, there, loc_s).start()
 
         by_array(i, go)
@@ -345,76 +450,91 @@
 
     @pl.when(is_in)
     def _():
-        def first(t, carry):
-            update(t)
+        def tick(t, carry):
+            @pl.when(t < PER)
+            def _():
+                update(t, order(t))
+
+            @pl.when((t >= LOCAL) & (t < LOCAL + PER))
+            def _():
+                pass_on(order(t - LOCAL), other, (0, t, end))
+
+            @pl.when((t >= PER) & (t < 2 * PER))
+            def _():
+                pass_on(t - PER, end, (1, t, other))
+
+            f = t - (LOCAL + PER)
+
+            @pl.when((f >= 0) & (f < PER - X))
+            def _():
+                pass_on(f, far, (0, t, end))
+
+            @pl.when(f >= PER - X)
+            def _():
+                pass_tail(f)
+
             return carry
 
-        lax.fori_loop(0, PER, first, 0)
-
-        def second(i, carry):
-            pass_on(i, other, (0, PER + i, end))
-            pass_on(i, end, (1, PER + i, other))
-            return carry
-
-        lax.fori_loop(0, PER, second, 0)
-
-        def third(i, carry):
-            pass_on(i, far, (0, 2 * PER + i, end))
-            return carry
-
-        lax.fori_loop(0, PER - X, third, 0)
-
-        def fourth(i, carry):
-            pass_tail(i)
-            return carry
-
-        lax.fori_loop(PER - X, PER, fourth, 0)
+        lax.fori_loop(0, LOCAL + 2 * PER, tick, 0)
 
     @pl.when(is_end)
     def _():
         def tick(t, carry):
             u = t + AHEAD
 
-            @pl.when(u < PER)
+            @pl.when(u < GUEST)
             def _():
                 send_sum(u)
 
+            @pl.when(t < 4)
+            def _():
+                share(4 + t)
+
             @pl.when(t < PER)
             def _():
-                update(t)
-
-            @pl.when((u >= PER) & (u < 2 * PER))
-            def _():
-                send_new(u - PER, u)
+                update(t, t)
+
+            @pl.when((u >= GUEST) & (u < GUEST + PER))
+            def _():
+                send_new(u - GUEST, u)
+
+            @pl.when((t >= PER) & (t < PER + GUEST))
+            def _():
+                update_guest(t)
 
             got = t - LAG
 
-            @pl.when((got >= 0) & (got < 3 * PER - X))
-            def _():
-                which = got // PER
-                pass_on(lax.rem(got, PER), jnp.where(which == 0, mine, jnp.where(which == 1, other, far)), None)
+            @pl.when((got >= 0) & (got < LOCAL + 2 * PER - X))
+            def _():
+                src = jnp.where(got < LOCAL, mine, jnp.where(got < LOCAL + PER, other, far))
+                i = jnp.where(got < LOCAL, GUEST + got, jnp.where(got < LOCAL + PER, order(got - LOCAL), got - LOCAL - PER))
+                pass_on(i, src, None)
 
             return carry
 
-        lax.fori_loop(0, 3 * PER - X + LAG, tick, 0)
+        lax.fori_loop(0, LOCAL + 2 * PER - X + LAG, tick, 0)
 
     for slot in range(2):
         wait(mq.at[slot], mv_s.at[slot, 0])
         wait(vq.at[slot], mv_s.at[slot, 1])
     six = gbuf.at[pl.ds(0, PER)]
-    wait(six, loc_s)
     for k in range(W):
         wait(gbuf.at[0], out_s.at[0, k])
 
     @pl.when(is_in)
     def _():
+        wait(six, loc_s)
+        wait(gbuf.at[pl.ds(0, 16)], pf_s)
         for k in range(W):
             wait(gbuf.at[0], out_s.at[1, k])
 
     @pl.when(is_end)
     def _():
-        for k in range(1, 8):
-            wait(nrm.at[slot_of], ns_s.at[k])
+        wait(gbuf.at[pl.ds(0, PER + GUEST)], loc_s)
+        wait(gbuf.at[pl.ds(0, 48)], pf_s)
+
+    for k in range(1, 8):
+        wait(nrm.at[d], ns_s.at[k])
 
     for k in range(4):
         less = is_end & (far == k)
@@ -527,9 +647,11 @@
                 pltpu.VMEM((2, S, *chunk), jnp.bfloat16),
                 pltpu.VMEM((2, S, *chunk), jnp.bfloat16),
                 pltpu.VMEM((2, S, *chunk), jnp.bfloat16),
+                pltpu.VMEM((LOCAL, *chunk), jnp.bfloat16),
+                pltpu.VMEM((GUEST, 2, *chunk), jnp.float32),
                 pltpu.VMEM((N, *chunk), jnp.bfloat16),
                 pltpu.VMEM((ROWS, CC), jnp.float32),
-                pltpu.VMEM((4, 8, 128), jnp.float32),
+                pltpu.VMEM((8, 8, 128), jnp.float32),
                 pltpu.VMEM((1, CC), jnp.float32),
                 pltpu.VMEM((2, *chunk), jnp.float32),
                 pltpu.VMEM((2, *chunk), jnp.float32),
@@ -544,6 +666,9 @@
                 regular((2,)),
                 regular((2,)),
                 dma((PER,)),
+                dma((LOCAL,)),
+                dma((GUEST, 2)),
+                dma,
                 dma((4, PER)),
                 dma((2, W)),
                 dma((4,)),
@@ -551,10 +676,10 @@
                 dma,
                 dma((2, 3)),
                 dma((2, 2)),
-                dma((4,)),
+                dma((8,)),
                 dma((8,)),
             ],
-            compiler_params=pltpu.CompilerParams(collective_id=0, has_side_effects=True, vmem_limit_bytes=40 * 2**20),
+            compiler_params=pltpu.CompilerParams(collective_id=0, has_side_effects=True, vmem_limit_bytes=54 * 2**20),
             cost_estimate=pl.CostEstimate(flops=10**9, bytes_accessed=3 * 10**8, transcendentals=3 * 2**20),
         )(*arrays)
         one = lax.ppermute(tail, "dp", [(2, 0), (3, 1), (4, 6), (5, 7)])

time: 740 us -> 696 us (0.941)
  Pallas kernels: 708 us -> 676 us
  waiting for transfers between devices: 20.8 us -> 3.82 us
    pallas_call x1, Pallas kernels: 656 us -> 624 us  [step(): pl.pallas_call(functools.partial(kernel, count), out_shape=[*out, last],...]
    ppermute x1, waiting for transfers between devices: 15.2 us -> 0.01 us  [step(): one = lax.ppermute(tail, 'dp', [(2, 0), (3, 1), (4, 6), (5, 7)])]
  transfers between devices with their start and end apart: 2 -> 2, of which waited for: 2 -> 1; matrix products, arithmetic and copies ran while one was open for 0% -> 0% of each run, Pallas kernels for 7% -> 7%
where the time goes in v4:
time: 696 us; the launch traced here: 695 us
  Pallas kernels  676 us (97%)
  local copies, waits for them, and re-layouts  10.9 us (2%)
    pallas_call x1, Pallas kernels, step(): pl.pallas_call(functools.partial(kernel, count), out_shape=[*out, last],...  624 us
    pallas_call x1, Pallas kernels, step(): pl.pallas_call(copies, out_shape=out, in_specs=[any_] * 9, out_specs=[any...  49.3 us
  transfers between devices with their start and end apart: 2, of which 1 were waited for; matrix products, arithmetic and copies ran while one was open for 0% of the time, Pallas kernels for 7%

profile of v4, /device:TPU:0, one launch (start us, length us, event | category | flops | bytes accessed | tf_op | source)
XLA Modules:
  0.0 695.0 jit_solution(15199831694837286018)
XLA Ops:
  0.6 624.4 %shard_map.187 = (bf16[2,1024,4096]{2,1,0:T(8,128)(2,1)}, bf16[2,1024,4096]{2,1,0:T(8,128)(2,1)}, bf16[2,4096,1024]{2,1,0:T(8,128)(2,1)}, f32[2,128,4096]{2,1,0:...) custom-call(bf16[1,2,1024,4096]{3,2,1,0:T(8,128)(2,1)} %refs_0_.1, ...), custom_call_target="tpu_custom_call" | custom-call | flops 1000000000 | bytes 300000000 | tf_op jit(solution)/shard_map/pallas_call | solution.py:640
  625.1 1.3 collective-permute-start
  626.4 0.0 copy-start
  626.4 2.2 copy-done
  628.5 0.0 copy-start.1
  628.5 2.2 copy-done.1
  630.7 0.0 copy-start.2
  630.7 2.2 copy-done.2
  632.9 0.0 copy-start.3
  632.9 2.2 copy-done.3
  635.1 0.0 copy-start.4
  635.1 2.2 copy-done.4
  637.3 0.0 copy-start.5
  637.3 49.3 %shard_map.188 = (bf16[2,1024,4096]{2,1,0:T(8,128)(2,1)}, bf16[2,1024,4096]{2,1,0:T(8,128)(2,1)}, bf16[2,4096,1024]{2,1,0:T(8,128)(2,1)}, f32[2,128,4096]{2,1,0:...) custom-call(bf16[2,1024,4096]{2,1,0:T(8,128)(2,1)} %get-tuple-elemen, ...), custom_call_target="tpu_custom_call" | custom-call | flops 400000000 | bytes 157286400 | tf_op jit(solution)/shard_map/pallas_call | solution.py:686
  686.6 0.0 collective-permute-done.one
  686.7 2.2 collective-permute-start.1
  688.9 3.8 collective-permute-done.1.two
  692.7 0.0 copy-done.5
  692.7 2.3 shard_map.189
Async XLA Ops:
  625.1 61.6 %collective-permute-start = (bf16[8,128,1024]{2,1,0:T(8,128)(2,1)}, bf16[8,128,1024]{2,1,0:T(8,128)(2,1)S(1)}, u32[]{:S(2)}, u32[]{:S(2)}) collective-permute-start(bf16[8,128,1024]{2,1,0:T(8,128)(2,1)} %get-tuple-element.41.tail), channel_id=1, source_target_pairs={{2,0},{3,1},{4,6},{5,7},{10,8},{11,9},{12,14},{13,15},{18,16},{19,... | collective-permute-start | bytes 6291464 | tf_op jit(solution)/shard_map/ppermute | solution.py:685
  626.4 2.2 copy-start
  628.5 2.2 copy-start.1
  630.7 2.2 copy-start.2
  632.9 2.2 copy-start.3
  635.1 2.2 copy-start.4
  637.3 55.4 %copy-start.5 = (bf16[8,128,1024]{2,1,0:T(8,128)(2,1)S(1)}, bf16[8,128,1024]{2,1,0:T(8,128)(2,1)}, u32[]{:S(2)}) copy-start(bf16[8,128,1024]{2,1,0:T(8,128)(2,1)} %get-tuple-element.41.tail) | copy-start | bytes 6291460
  686.7 6.1 collective-permute-start.1

commit v5 on v4

--- a/solution.py
+++ b/solution.py
@@ -13,12 +13,16 @@
 PER = 24
 N = 2 * PER
 S = 4
+U = 8
 LOCAL = 8
 GUEST = PER - LOCAL
 D = 2
 W = 3
-AHEAD = 2 * D
+PAUSE = D + 2
+STEPS = N + 2 * D + PAUSE
+AHEAD = 2
 LAG = 3
+COPIES, LOOK = 6, 4
 X = 8
 ROWS = 16
 
@@ -60,11 +64,9 @@
     buddy = {"dp": partner}
 
     def chunk_of(s, n):
-        zz = z if s == 0 else 3 - z
-        m = jnp.where(zz == 3, jnp.where(n < 4, N - LOCAL + n, jnp.where(n < N - 4, n - 4, n)), n)
-        late = m >= N - LOCAL
-        b = jnp.where((m >= GUEST) & jnp.logical_not(late), 1, 0)
-        i = jnp.where(late, m - (N - PER), m - b * GUEST)
+        late = n >= N - LOCAL
+        b = jnp.where((n >= GUEST) & jnp.logical_not(late), 1, 0)
+        i = jnp.where(late, n - (N - PER), n - b * GUEST)
         return (2 + b if s == 0 else 1 - b), b, i
 
     def block(ref, a, layer, q):
@@ -129,26 +131,29 @@
         zz = z if s == 0 else 3 - z
         down = z + 1 if s == 0 else z - 1
         above = z - 1 if s == 0 else z + 1
-        j = k - jnp.where(zz == 3, 3 * D - 4, D * zz)
-
-        @pl.when((j >= 0) & (j < N))
-        def _():
-            slot = lax.rem(j, S)
+        j = k - D * zz
+        pause = (zz == 2) & (j >= N - LOCAL)
+        held = pause & (j < N - LOCAL + PAUSE)
+        j = j - jnp.where(pause, PAUSE, 0)
+
+        @pl.when((j >= 0) & (j < N) & jnp.logical_not(held))
+        def _():
+            slot, place_ = lax.rem(j, S), lax.rem(j, U)
             _, b, i = chunk_of(s, j)
-            back = (zz == 3) & ((j < 4) | (j >= N - 4))
+            back = (zz == 3) & (j >= N - LOCAL)
             here = (zz == 2) & (j >= N - LOCAL)
             root = (zz == 3) & jnp.logical_not(back)
             on = (zz < 3) & jnp.logical_not(here)
             wait(own.at[s, slot], own_s.at[s, slot])
             wait(par.at[s, slot], par_s.at[s, slot])
 
-            @pl.when((on & (j >= S)) | (back & (j >= N - 4)))
+            @pl.when((on & (j >= S)) | (back & (j >= N - LOCAL + S)))
             def _():
                 wait(snd.at[s, slot], snd_s.at[s, slot])
 
             @pl.when((zz > 0) & jnp.logical_not(back))
             def _():
-                wait(up.at[s, slot], up_s.at[s, slot])
+                wait(up.at[s, place_], up_s.at[s, place_])
 
             def two(r):
                 return f32(own[s, slot, r, :]) + f32(par[s, slot, r, :])
@@ -163,7 +168,7 @@
             @pl.when((zz > 0) & on)
             def _():
                 def add(r):
-                    snd[s, slot, r, :] = (f32(up[s, slot, r, :]) + two(r)).astype(jnp.bfloat16)
+                    snd[s, slot, r, :] = (f32(up[s, place_, r, :]) + two(r)).astype(jnp.bfloat16)
 
                 rows(add)
 
@@ -174,19 +179,19 @@
 
             @pl.when(root)
             def _():
-                rows(lambda r: keep(r, f32(up[s, slot, r, :]) + two(r)))
+                rows(lambda r: keep(r, f32(up[s, place_, r, :]) + two(r)))
 
             @pl.when(here)
             def _():
                 e = i - GUEST
                 wait(ext.at[e], ext_s.at[e])
-                rows(lambda r: keep(r, f32(up[s, slot, r, :]) + two(r) + f32(ext[e, r, :])))
+                rows(lambda r: keep(r, f32(up[s, place_, r, :]) + two(r) + f32(ext[e, r, :])))
 
             @pl.when(j < N - S)
             def _():
                 pl.semaphore_signal(par_c.at[s], inc=1, device_id=buddy, device_id_type=MESH)
 
-            @pl.when(((zz > 0) & (zz < 3) & (j < N - S)) | (root & (j < N - LOCAL + 4 - S)))
+            @pl.when(((zz > 0) & (zz < 3) & (j < N - U)) | (root & (j < N - LOCAL - U)))
             def _():
                 pl.semaphore_signal(up_c.at[s], inc=1, device_id=dev(above), device_id_type=MESH)
 
@@ -196,11 +201,11 @@
 
             @pl.when(on)
             def _():
-                @pl.when(j >= S)
+                @pl.when(j >= U)
                 def _():
                     pl.semaphore_wait(up_c.at[s], 1)
 
-                remote(snd.at[s, slot], up.at[s, slot], snd_s.at[s, slot], up_s.at[s, slot], dev(down)).start()
+                remote(snd.at[s, slot], up.at[s, place_], snd_s.at[s, slot], up_s.at[s, place_], dev(down)).start()
 
             @pl.when(back)
             def _():
@@ -241,28 +246,28 @@
         remote(gbuf.at[u], gbuf.at[u], out_s.at[0, lax.rem(u, W)], g_s.at[u], dev(mine)).start()
 
     def step(k, carry):
-        @pl.when(is_in & (k < 4))
+        @pl.when(is_in & (k < 2))
         def _():
             bring(k)
 
         process(0, k)
         process(1, k)
 
-        @pl.when(is_in & (k >= N - 4) & (k < N))
-        def _():
-            bring(k - (N - 8))
-
-        @pl.when(is_end & (k >= 4) & (k < 8))
-        def _():
-            share(k - 4)
-
-        @pl.when(is_end & (k >= N))
-        def _():
-            send_sum(k - N)
+        @pl.when(is_in & (k >= N - 4) & (k < N + 2))
+        def _():
+            bring(k - (N - 6))
+
+        @pl.when(is_end & ((k == 6) | (k == 7)))
+        def _():
+            share(k - 6)
+
+        @pl.when(is_end & (k >= STEPS - AHEAD))
+        def _():
+            send_sum(k - (STEPS - AHEAD))
 
         return carry
 
-    lax.fori_loop(0, N + 2 * D, step, 0)
+    lax.fori_loop(0, STEPS, step, 0)
 
     def order(t):
         return jnp.where(t < LOCAL, GUEST + t, t - LOCAL)
@@ -486,9 +491,9 @@
             def _():
                 send_sum(u)
 
-            @pl.when(t < 4)
-            def _():
-                share(4 + t)
+            @pl.when(t < 6)
+            def _():
+                share(2 + t)
 
             @pl.when(t < PER)
             def _():
@@ -563,7 +568,7 @@
     used = [[0] * 4, []]
     slots = []
     for it in items:
-        slots.append(used[0][it[1]] % 3)
+        slots.append(used[0][it[1]] % COPIES)
         used[0][it[1]] += 1
     last = {}
 
@@ -583,13 +588,13 @@
         a, kind, layer, r, size = items[k]
         return pltpu.make_async_copy(buf[kind].at[slots[k]], dst[a].at[layer, pl.ds(r, size)], sem_out.at[kind, slots[k]])
 
-    for k in range(2):
+    for k in range(LOOK):
         start_in(k)
     for k in range(n):
         inn(k).wait()
         out(k).start()
-        if k + 2 < n:
-            start_in(k + 2)
+        if k + LOOK < n:
+            start_in(k + LOOK)
     for k in last.values():
         out(k).wait()
 
@@ -645,7 +650,7 @@
             scratch_shapes=[
                 pltpu.VMEM((2, S, *chunk), jnp.bfloat16),
                 pltpu.VMEM((2, S, *chunk), jnp.bfloat16),
-                pltpu.VMEM((2, S, *chunk), jnp.bfloat16),
+                pltpu.VMEM((2, U, *chunk), jnp.bfloat16),
                 pltpu.VMEM((2, S, *chunk), jnp.bfloat16),
                 pltpu.VMEM((LOCAL, *chunk), jnp.bfloat16),
                 pltpu.VMEM((GUEST, 2, *chunk), jnp.float32),
@@ -661,7 +666,7 @@
                 dma((2, S)),
                 dma((2, S)),
                 dma((2, S)),
-                dma((2, S)),
+                dma((2, U)),
                 dma((2, S)),
                 regular((2,)),
                 regular((2,)),
@@ -689,14 +694,14 @@
             in_specs=[any_] * 9,
             out_specs=[any_] * 9,
             scratch_shapes=[
-                pltpu.VMEM((3, 256, 4096), jnp.bfloat16),
-                pltpu.VMEM((3, 1024, 1024), jnp.bfloat16),
-                pltpu.VMEM((3, 128, 4096), jnp.float32),
-                pltpu.VMEM((3, 512, 1024), jnp.float32),
-                dma((4, 3)),
-                dma((4, 3)),
+                pltpu.VMEM((COPIES, 256, 4096), jnp.bfloat16),
+                pltpu.VMEM((COPIES, 1024, 1024), jnp.bfloat16),
+                pltpu.VMEM((COPIES, 128, 4096), jnp.float32),
+                pltpu.VMEM((COPIES, 512, 1024), jnp.float32),
+                dma((4, COPIES)),
+                dma((4, COPIES)),
             ],
-            compiler_params=pltpu.CompilerParams(vmem_limit_bytes=32 * 2**20),
+            compiler_params=pltpu.CompilerParams(vmem_limit_bytes=63 * 2**20),
             cost_estimate=pl.CostEstimate(flops=4 * 10**8, bytes_accessed=150 * 2**20, transcendentals=0),
         )(*first)
         one, *copied = lax.optimization_barrier((one, *copied))

time: 696 us -> 676 us (0.971)
  Pallas kernels: 676 us -> 666 us
  local copies, waits for them, and re-layouts: 10.9 us -> 1.59 us
    pallas_call x1, Pallas kernels: 624 us -> 613 us  [step(): pl.pallas_call(functools.partial(kernel, count), out_shape=[*out, last],...]
    unnamed x12 -> x2, local copies, waits for them, and re-layouts: 10.9 us -> 1.59 us
where the time goes in v5:
time: 676 us
  Pallas kernels  666 us (99%)
    pallas_call x1, Pallas kernels, step(): pl.pallas_call(functools.partial(kernel, count), out_shape=[*out, last],...  613 us
    pallas_call x1, Pallas kernels, step(): pl.pallas_call(copies, out_shape=out, in_specs=[any_] * 9, out_specs=[any...  49.6 us
  transfers between devices with their start and end apart: 2, of which 1 were waited for; matrix products, arithmetic and copies ran while one was open for 0% of the time, Pallas kernels for 7%

profile of v5, /device:TPU:0, one launch (start us, length us, event | category | flops | bytes accessed | tf_op | source)
XLA Modules:
  0.0 675.8 jit_solution(11222679381812208286)
XLA Ops:
  0.6 613.0 %shard_map.187 = (bf16[2,1024,4096]{2,1,0:T(8,128)(2,1)}, bf16[2,1024,4096]{2,1,0:T(8,128)(2,1)}, bf16[2,4096,1024]{2,1,0:T(8,128)(2,1)}, f32[2,128,4096]{2,1,0:...) custom-call(bf16[1,2,1024,4096]{3,2,1,0:T(8,128)(2,1)} %refs_0_.1, ...), custom_call_target="tpu_custom_call" | custom-call | flops 1000000000 | bytes 300000000 | tf_op jit(solution)/shard_map/pallas_call | solution.py:645
  613.6 1.3 collective-permute-start
  614.9 49.6 %shard_map.188 = (bf16[2,1024,4096]{2,1,0:T(8,128)(2,1)}, bf16[2,1024,4096]{2,1,0:T(8,128)(2,1)}, bf16[2,4096,1024]{2,1,0:T(8,128)(2,1)}, f32[2,128,4096]{2,1,0:...) custom-call(bf16[2,1024,4096]{2,1,0:T(8,128)(2,1)} %get-tuple-elemen, ...), custom_call_target="tpu_custom_call" | custom-call | flops 400000000 | bytes 157286400 | tf_op jit(solution)/shard_map/pallas_call | solution.py:691
  664.5 0.0 collective-permute-done.one
  664.6 2.2 collective-permute-start.1
  666.8 3.8 collective-permute-done.1.two
  670.6 0.0 copy-start
  670.6 1.6 copy-done
  672.2 3.6 shard_map.189
Async XLA Ops:
  613.6 50.9 %collective-permute-start = (bf16[8,128,1024]{2,1,0:T(8,128)(2,1)}, bf16[8,128,1024]{2,1,0:T(8,128)(2,1)}, u32[]{:S(2)}, u32[]{:S(2)}) collective-permute-start(bf16[8,128,1024]{2,1,0:T(8,128)(2,1)} %get-tuple-element.41.tail), channel_id=1, source_target_pairs={{2,0},{3,1},{4,6},{5,7},{10,8},{11,9},{12,14},{13,15},{18,16},{19,... | collective-permute-start | bytes 6291464 | tf_op jit(solution)/shard_map/ppermute | solution.py:690
  664.6 6.1 collective-permute-start.1
  670.6 1.6 copy-start

commit v6 on v5

--- a/solution.py
+++ b/solution.py
@@ -112,8 +112,7 @@
     pl.semaphore_wait(barrier, 10)
 
     for s in range(2):
-        for j in range(S):
-            start_give(s, jnp.int32(j))
+        start_give(s, jnp.int32(0))
 
     acc[...] = jnp.zeros_like(acc)
 
@@ -252,6 +251,12 @@
 
         process(0, k)
         process(1, k)
+
+        @pl.when(k == 0)
+        def _():
+            for s in range(2):
+                for j in range(1, S):
+                    start_give(s, jnp.int32(j))
 
         @pl.when(is_in & (k >= N - 4) & (k < N + 2))
         def _():
@@ -599,38 +604,35 @@
         out(k).wait()
 
 
-def place(tail, one, two, *refs):
-    dst, buf, sem_in, sem_out = refs[3:6], refs[6], refs[7], refs[8]
+def place(n, *refs):
+    src, dst, buf, sem_in, sem_out = refs[:n], refs[n + 3 : n + 6], refs[n + 6], refs[n + 7], refs[n + 8]
     d = lax.axis_index("dp")
     z, c = d // 2, d % 2
     is_in = (z == 1) | (z == 2)
     far = jnp.where(z >= 2, 0, 3)
 
-    @pl.when(is_in)
-    def _():
-        pltpu.make_async_copy(tail, buf.at[0], sem_in.at[0]).start()
+    def put(ref, core):
+        half = X // 2
+        parts = [pl.ds(0, half), pl.ds(half, X - half)]
+        for h, part in enumerate(parts):
+            pltpu.make_async_copy(ref.at[part], buf.at[part], sem_in.at[h]).start()
+        for h, part in enumerate(parts):
+            pltpu.make_async_copy(ref.at[part], buf.at[part], sem_in.at[h]).wait()
+            for k in range(part.start, part.start + part.size):
+                i = PER - X + k
+                a = i // 8
+                there = whole(dst[a], a, (i % 8) // 4, i % 4, 2 * far + core)
+                pltpu.make_async_copy(buf.at[k], there, sem_out).start()
+        pltpu.make_async_copy(buf, buf, sem_out).wait()
+
+    if n == 2:
+        @pl.when(is_in)
+        def _():
+            put(src[0], c)
 
     @pl.when(jnp.logical_not(is_in))
     def _():
-        pltpu.make_async_copy(one, buf.at[0], sem_in.at[0]).start()
-        pltpu.make_async_copy(two, buf.at[1], sem_in.at[1]).start()
-
-    def put(which, core):
-        pltpu.make_async_copy(one, buf.at[which], sem_in.at[which]).wait()
-        for k in range(X):
-            i = PER - X + k
-            a = i // 8
-            there = whole(dst[a], a, (i % 8) // 4, i % 4, 2 * far + core)
-            pltpu.make_async_copy(buf.at[which, k], there, sem_out.at[which]).start()
-
-    put(0, c)
-
-    @pl.when(jnp.logical_not(is_in))
-    def _():
-        put(1, 1 - c)
-        pltpu.make_async_copy(one, buf.at[1], sem_out.at[1]).wait()
-
-    pltpu.make_async_copy(one, buf.at[0], sem_out.at[0]).wait()
+        put(src[-1], c if n == 2 else 1 - c)
 
 
 def solution(mesh):
@@ -706,15 +708,19 @@
         )(*first)
         one, *copied = lax.optimization_barrier((one, *copied))
         two = lax.ppermute(one, "dp", [(0, 1), (1, 0), (6, 7), (7, 6)])
-        new = pl.pallas_call(
-            place,
-            out_shape=out[:3],
-            in_specs=[any_] * 6,
-            out_specs=[any_] * 3,
-            input_output_aliases={3: 0, 4: 1, 5: 2},
-            scratch_shapes=[pltpu.VMEM((2, X, *chunk), jnp.bfloat16), dma((2,)), dma((2,))],
-            compiler_params=pltpu.CompilerParams(vmem_limit_bytes=16 * 2**20),
-        )(tail, one, two, *copied[:3])
+        new = copied[:3]
+        for held in ((tail, one), (two,)):
+            n = len(held)
+            new = pl.pallas_call(
+                functools.partial(place, n),
+                out_shape=out[:3],
+                in_specs=[any_] * (n + 3),
+                out_specs=[any_] * 3,
+                input_output_aliases={n: 0, n + 1: 1, n + 2: 2},
+                scratch_shapes=[pltpu.VMEM((X, *chunk), jnp.bfloat16), dma((2,)), dma],
+                compiler_params=pltpu.CompilerParams(vmem_limit_bytes=63 * 2**20),
+                cost_estimate=pl.CostEstimate(flops=10**7, bytes_accessed=4 * 2**20, transcendentals=0),
+            )(*held, *new)
         return (*new, *copied[3:])
 
     all_of, cut = P(None, None, None), P(None, "dp", None)

time: 676 us -> 672 us (level)
  transfers between devices with their start and end apart: 2 -> 2, of which waited for: 1 -> 1; matrix products, arithmetic and copies ran while one was open for 0% -> 0% of each run, Pallas kernels for 7% -> 8%
where the time goes in v6:
time: 672 us
  Pallas kernels  667 us (99%)
    pallas_call x1, Pallas kernels, step(): pl.pallas_call(functools.partial(kernel, count), out_shape=[*out, last],...  612 us
    pallas_call x1, Pallas kernels, step(): pl.pallas_call(copies, out_shape=out, in_specs=[any_] * 9, out_specs=[any...  49.6 us
  transfers between devices with their start and end apart: 2, of which 1 were waited for; matrix products, arithmetic and copies ran while one was open for 0% of the time, Pallas kernels for 8%

profile of v6, /device:TPU:0, one launch (start us, length us, event | category | flops | bytes accessed | tf_op | source)
XLA Modules:
  0.0 672.0 jit_solution(1584525440790598205)
XLA Ops:
  0.6 611.8 %shard_map.187 = (bf16[2,1024,4096]{2,1,0:T(8,128)(2,1)}, bf16[2,1024,4096]{2,1,0:T(8,128)(2,1)}, bf16[2,4096,1024]{2,1,0:T(8,128)(2,1)}, f32[2,128,4096]{2,1,0:...) custom-call(bf16[1,2,1024,4096]{3,2,1,0:T(8,128)(2,1)} %refs_0_.1, ...), custom_call_target="tpu_custom_call" | custom-call | flops 1000000000 | bytes 300000000 | tf_op jit(solution)/shard_map/pallas_call | solution.py:647
  612.5 1.3 collective-permute-start
  613.8 49.6 %shard_map.188 = (bf16[2,1024,4096]{2,1,0:T(8,128)(2,1)}, bf16[2,1024,4096]{2,1,0:T(8,128)(2,1)}, bf16[2,4096,1024]{2,1,0:T(8,128)(2,1)}, f32[2,128,4096]{2,1,0:...) custom-call(bf16[2,1024,4096]{2,1,0:T(8,128)(2,1)} %get-tuple-elemen, ...), custom_call_target="tpu_custom_call" | custom-call | flops 400000000 | bytes 157286400 | tf_op jit(solution)/shard_map/pallas_call | solution.py:693
  663.4 0.0 collective-permute-done.refs_1_
  663.4 2.2 collective-permute-start.1
  665.7 2.6 shard_map.189
  668.3 1.2 collective-permute-done.1.refs_0_
  669.4 2.6 shard_map.190
Async XLA Ops:
  612.5 50.9 %collective-permute-start = (bf16[8,128,1024]{2,1,0:T(8,128)(2,1)}, bf16[8,128,1024]{2,1,0:T(8,128)(2,1)}, u32[]{:S(2)}, u32[]{:S(2)}) collective-permute-start(bf16[8,128,1024]{2,1,0:T(8,128)(2,1)} %get-tuple-element.44.refs_0_), channel_id=1, source_target_pairs={{2,0},{3,1},{4,6},{5,7},{10,8},{11,9},{12,14},{13,15},{18,16},{19,... | collective-permute-start | bytes 6291464 | tf_op jit(solution)/shard_map/ppermute | solution.py:692
  663.4 6.0 collective-permute-start.1

commit v7 on v6

--- a/solution.py
+++ b/solution.py
@@ -18,7 +18,7 @@
 GUEST = PER - LOCAL
 D = 2
 W = 3
-PAUSE = D + 2
+PAUSE = D + 1
 STEPS = N + 2 * D + PAUSE
 AHEAD = 2
 LAG = 3

time: 672 us -> 672 us (level)
  no operation moved by 1% of the time
where the time goes in v7:
time: 672 us
  Pallas kernels  667 us (99%)
    pallas_call x1, Pallas kernels, step(): pl.pallas_call(functools.partial(kernel, count), out_shape=[*out, last],...  612 us
    pallas_call x1, Pallas kernels, step(): pl.pallas_call(copies, out_shape=out, in_specs=[any_] * 9, out_specs=[any...  49.6 us
  transfers between devices with their start and end apart: 2, of which 1 were waited for; matrix products, arithmetic and copies ran while one was open for 0% of the time, Pallas kernels for 8%

profile of v7, /device:TPU:0, one launch (start us, length us, event | category | flops | bytes accessed | tf_op | source)
XLA Modules:
  0.0 672.0 jit_solution(12332071978505151657)
XLA Ops:
  0.6 611.8 %shard_map.187 = (bf16[2,1024,4096]{2,1,0:T(8,128)(2,1)}, bf16[2,1024,4096]{2,1,0:T(8,128)(2,1)}, bf16[2,4096,1024]{2,1,0:T(8,128)(2,1)}, f32[2,128,4096]{2,1,0:...) custom-call(bf16[1,2,1024,4096]{3,2,1,0:T(8,128)(2,1)} %refs_0_.1, ...), custom_call_target="tpu_custom_call" | custom-call | flops 1000000000 | bytes 300000000 | tf_op jit(solution)/shard_map/pallas_call | solution.py:647
  612.5 1.3 collective-permute-start
  613.8 49.6 %shard_map.188 = (bf16[2,1024,4096]{2,1,0:T(8,128)(2,1)}, bf16[2,1024,4096]{2,1,0:T(8,128)(2,1)}, bf16[2,4096,1024]{2,1,0:T(8,128)(2,1)}, f32[2,128,4096]{2,1,0:...) custom-call(bf16[2,1024,4096]{2,1,0:T(8,128)(2,1)} %get-tuple-elemen, ...), custom_call_target="tpu_custom_call" | custom-call | flops 400000000 | bytes 157286400 | tf_op jit(solution)/shard_map/pallas_call | solution.py:693
  663.4 0.0 collective-permute-done.refs_1_
  663.4 2.2 collective-permute-start.1
  665.7 2.6 shard_map.189
  668.3 1.2 collective-permute-done.1.refs_0_
  669.4 2.6 shard_map.190
Async XLA Ops:
  612.5 50.9 %collective-permute-start = (bf16[8,128,1024]{2,1,0:T(8,128)(2,1)}, bf16[8,128,1024]{2,1,0:T(8,128)(2,1)}, u32[]{:S(2)}, u32[]{:S(2)}) collective-permute-start(bf16[8,128,1024]{2,1,0:T(8,128)(2,1)} %get-tuple-element.44.refs_0_), channel_id=1, source_target_pairs={{2,0},{3,1},{4,6},{5,7},{10,8},{11,9},{12,14},{13,15},{18,16},{19,... | collective-permute-start | bytes 6291464 | tf_op jit(solution)/shard_map/ppermute | solution.py:692
  663.4 6.0 collective-permute-start.1
